TPU v7x, 128 devices: a whole 4x4x4 slice. The times are simulated.
128 devices in a mesh: seq: 32 (over y, z, core), batch: 4 (over x).
Axes of the slice: x: 4, y: 4, z: 4, core: 2. Of those that a mesh axis runs over, the one named last changes fastest.
Arguments:
- queries: bfloat16 [4, 4096, 4096], P('batch', 'seq'), may hold values from -130 to 130
- keys: bfloat16 [4, 4096, 1024], P('batch', 'seq'), may hold values from -4 to 4
- values: bfloat16 [4, 4096, 1024], P('batch', 'seq'), may hold values from -4 to 4
- lengths: int32 [4], P('batch'), may hold values from 2048 to 4096
- block_pos: int32 [4, 32], P('batch'), may hold values from 0 to 31, each once within a row
- w_in: bfloat16 [6144, 1024], replicated, may hold values from -0.078125 to 0.078125
- b_in: float32 [1024], replicated, may hold values from -3 to 3
- output_weight: bfloat16 [1024, 8], replicated, may hold values from -0.1875 to 0.1875
- output_bias: float32 [8], replicated, may hold values from 1 to 2
Outputs:
- grad_w_in: float32 [6144, 1024], P(('seq', 'batch'))
- grad_b_in: float32 [1024], replicated
- output_weight_gradient: float32 [1024, 8], replicated
- output_bias_gradient: float32 [8], replicated
Inputs may be any that keep to these rules, and one draw needn't show every extreme that they name: Each row of block_pos names every block 0 to 31 once.
All inputs are finite; a program needn't handle non-finite values.
Results may differ from a plain program's by a relative error of at most 0.0017.
The roundings to bfloat16 on the way count: a program that leaves them out, or rounds other values in their place, can miss the bound.
Values may be sent and summed in bfloat16 or wider, within the bound.
A program may use at most 128 MiB of HBM per device.

v0:
```python
import math

import jax
import jax.numpy as jnp
from jax import lax
from jax.sharding import PartitionSpec as P


def split_up(array, dim, size):
    before, after = (array.shape[:dim], array.shape[dim + 1 :])
    return jnp.moveaxis(array.reshape(*before, size, -1, *after), dim, 0)


def sent_and_summed(array, axis, dim):
    size = lax.axis_size(axis)
    tiles = lax.all_to_all(split_up(array, dim, size), axis, 0, 0, tiled=True)
    return jnp.sum(tiles, axis=0)


def in_one(arrays, axis):
    ends = [0]
    for a in arrays:
        ends.append(ends[-1] + a.size)
    so_far = lax.psum(jnp.concatenate([a.ravel() for a in arrays]), axis)
    return tuple((so_far[b:e].reshape(a.shape) for a, b, e in zip(arrays, ends, ends[1:])))


def on_device(queries, keys, values, lengths, block_pos, w_in, b_in, output_weight, output_bias):
    q_rows = queries[0]
    k_rows = keys[0]
    v_rows = values[0]
    rows = q_rows.shape[0]
    heads_kv = output_weight.shape[1]
    head_size = k_rows.shape[1] // heads_kv
    group_index = q_rows.shape[1] // k_rows.shape[1]
    scale = 1.0 / math.sqrt(head_size)
    every_key = lax.all_gather(k_rows, "seq", axis=0, tiled=True)
    total = every_key.shape[0]
    order = block_pos[0]
    offsets = jnp.arange(rows, dtype=jnp.int32)
    key_pos = (order[:, None] * rows + offsets[None, :]).reshape(-1)
    mine = lax.axis_index("seq")
    query_pos = lax.dynamic_index_in_dim(order, mine, 0, keepdims=False) * rows + offsets
    limit = lengths[0]
    allowed = (key_pos[None, :] <= query_pos[:, None]) & (key_pos < limit)[None, :]
    query_live = (query_pos < limit).astype(jnp.float32)

    def group_mass(index, sums):
        q_part = lax.dynamic_slice_in_dim(
            q_rows, index * group_index * head_size, group_index * head_size, 1
        )
        q_part = q_part.reshape(rows, group_index, head_size)
        k_part = lax.dynamic_slice_in_dim(every_key, index * head_size, head_size, 1)
        scores = (
            jnp.einsum("qhd,kd->hqk", q_part, k_part, preferred_element_type=jnp.float32) * scale
        )
        masked = jnp.where(allowed[None], scores, -1e30)
        top = jnp.max(masked, axis=2, keepdims=True)
        weights = jnp.where(allowed[None], jnp.exp(masked - top), 0.0)
        denom = jnp.sum(weights, axis=2, keepdims=True)
        share = weights / denom * query_live[None, :, None]
        column = jnp.sum(share, axis=(0, 1))
        return lax.dynamic_update_index_in_dim(sums, column, index, 0)

    partial_value = lax.fori_loop(
        0, heads_kv, group_mass, jnp.zeros((heads_kv, total), jnp.float32)
    )
    mass = sent_and_summed(partial_value, "seq", 1)
    labels = jnp.log1p(mass).T
    features = jnp.concatenate([q_rows, k_rows, v_rows], axis=1)
    pre = jnp.dot(features, w_in, preferred_element_type=jnp.float32) + b_in
    act = jax.nn.silu(pre).astype(jnp.bfloat16)
    pred = jnp.dot(act, output_weight, preferred_element_type=jnp.float32) + output_bias
    norm = 1.0 / math.sqrt(lax.axis_size("batch") * total)
    resid = ((pred - labels) * query_live[:, None] * norm).astype(jnp.bfloat16)
    back = lax.dot_general(
        resid, output_weight, (((1,), (1,)), ((), ())), preferred_element_type=jnp.float32
    )
    sig = jax.nn.sigmoid(pre)
    delta = (back * sig * (1.0 + pre * (1.0 - sig))).astype(jnp.bfloat16)
    out_term = lax.dot_general(
        act, resid, (((0,), (0,)), ((), ())), preferred_element_type=jnp.float32
    )
    grad_b_in, output_weight_gradient, output_bias_gradient = in_one(
        (
            jnp.sum(delta.astype(jnp.float32), axis=0),
            out_term,
            jnp.sum(resid.astype(jnp.float32), axis=0),
        ),
        ("seq", "batch"),
    )
    grad_w_in = lax.psum_scatter(
        lax.dot_general(
            features, delta, (((0,), (0,)), ((), ())), preferred_element_type=jnp.float32
        ),
        ("seq", "batch"),
        scatter_dimension=0,
        tiled=True,
    )
    return (grad_w_in, grad_b_in, output_weight_gradient, output_bias_gradient)


def solution(mesh):
    return jax.shard_map(
        on_device,
        mesh=mesh,
        in_specs=(
            P("batch", "seq", None),
            P("batch", "seq", None),
            P("batch", "seq", None),
            P("batch"),
            P("batch", None),
            P(),
            P(),
            P(),
            P(),
        ),
        out_specs=(P(("seq", "batch"), None), P(), P(), P()),
        check_vma=False,
    )
```

profile of v0, /device:TPU:1, one launch (start us, length us, event | category | flops | bytes accessed | tf_op | source)
XLA Modules:
  0.0 517.5 jit_solution(12301234503528148574)
XLA Ops:
  7.2 0.7 all-gather.3.cloned.1.call-update
  7.9 1.1 copy.15
  9.7 1.1 copy.16
  10.8 1.6 copy.14
  12.5 1.2 fusion.51
  13.7 0.6 iota_add_fusion
  14.4 0.7 multiply_bitcast_fusion
  15.2 51.6 %all-gather.3.cloned.1.call-done = bf16[1,4096,1024]{2,1,0:T(8,128)(2,1)} async-done(((bf16[1,128,1024]{2,1,0:T(8,128)(2,1)}), bf16[1,4096,1024]{2,1,0:T(8,128)(2,1)}) %all-gather.3.cloned.1.call-update) | async-done | bytes 8388624 | tf_op jit(solution)/shard_map/all_gather | solution.py:37
  66.8 170.6 %while.16 = (s32[]{:T(128)}, f32[8,4096]{1,0:T(8,128)}, bf16[4096,1024]{1,0:T(8,128)(2,1)}, bf16[128,4096]{0,1:T(8,128)(2,1)S(1)}, s32[128]{0:T(128)S(1)}, /*ind...) while((s32[]{:T(128)}, f32[8,4096]{1,0:T(8,128)}, ...), condition=%wide.region_4.5_spmd.clone, body=%wide.region_0.4_spmd.clone.sunk | while | flops 1097869184 | bytes 22091528 | solution.py:65
  66.8 1.3 compare_convert_fusion.3
  68.1 1.4 compare_and_fusion.2
  69.5 8.6 %fusion.72 = f32[4,128,4096]{1,2,0:T(8,128)} fusion(pred[128,4096]{0,1:T(8,128)(4,1)S(1)} %compare_and_fusion.2, bf16[128,4,128]{0,2,1:T(8,128)(2,1)S(1)} %bitcast.69, bf16[4096,1024]{1,0:T(8,128)(2,1)} %get-tuple-element.300, s32[]{:T(128)S(6)} %select_n.79), kind=kOutput, calls=%fused_computation.2.clone.1 | convolution fusion | flops 545268736 | bytes 10616836 | tf_op jit(solution)/shard_map/while/body/eval_jaxpr/div | solution.py:61
  78.1 8.4 %multiply_reduce_fusion.2 = f32[4096]{0:T(1024)S(1)} fusion(f32[4,128,4096]{1,2,0:T(8,128)} %fusion.72, f32[128]{0:T(128)S(1)} %compare_convert_fusion.3, pred[128,4096]{0,1:T(8,128)(4,1)S(1)} %compare_and_fusion.2, bf16[128,4,128]{0,2,1:T(8,128)(2,1)S(1)} %bitcast.70, bf16[4096,1024]{1,0:T(8,128)(2,1)} %get-tuple-element.300, s32[]{:T(128)S(6)} %select_n.79), kind=kOutput, calls=%fused_computation.5.clone.1 | convolution fusion | flops 551551488 | bytes 10633732 | tf_op jit(solution)/shard_map/while/body/eval_jaxpr/sub | solution.py:59
  86.5 1.6 dynamic_update_slice.13
  88.1 1.3 compare_convert_fusion.3
  89.4 1.4 compare_and_fusion.2
  90.8 8.6 %fusion.72 = f32[4,128,4096]{1,2,0:T(8,128)} fusion(pred[128,4096]{0,1:T(8,128)(4,1)S(1)} %compare_and_fusion.2, bf16[128,4,128]{0,2,1:T(8,128)(2,1)S(1)} %bitcast.69, bf16[4096,1024]{1,0:T(8,128)(2,1)} %get-tuple-element.300, s32[]{:T(128)S(6)} %select_n.79), kind=kOutput, calls=%fused_computation.2.clone.1 | convolution fusion | flops 545268736 | bytes 10616836 | tf_op jit(solution)/shard_map/while/body/eval_jaxpr/div | solution.py:61
  99.4 8.4 %multiply_reduce_fusion.2 = f32[4096]{0:T(1024)S(1)} fusion(f32[4,128,4096]{1,2,0:T(8,128)} %fusion.72, f32[128]{0:T(128)S(1)} %compare_convert_fusion.3, pred[128,4096]{0,1:T(8,128)(4,1)S(1)} %compare_and_fusion.2, bf16[128,4,128]{0,2,1:T(8,128)(2,1)S(1)} %bitcast.70, bf16[4096,1024]{1,0:T(8,128)(2,1)} %get-tuple-element.300, s32[]{:T(128)S(6)} %select_n.79), kind=kOutput, calls=%fused_computation.5.clone.1 | convolution fusion | flops 551551488 | bytes 10633732 | tf_op jit(solution)/shard_map/while/body/eval_jaxpr/sub | solution.py:59
  107.8 1.6 dynamic_update_slice.13
  109.4 1.3 compare_convert_fusion.3
  110.8 1.4 compare_and_fusion.2
  112.2 8.6 %fusion.72 = f32[4,128,4096]{1,2,0:T(8,128)} fusion(pred[128,4096]{0,1:T(8,128)(4,1)S(1)} %compare_and_fusion.2, bf16[128,4,128]{0,2,1:T(8,128)(2,1)S(1)} %bitcast.69, bf16[4096,1024]{1,0:T(8,128)(2,1)} %get-tuple-element.300, s32[]{:T(128)S(6)} %select_n.79), kind=kOutput, calls=%fused_computation.2.clone.1 | convolution fusion | flops 545268736 | bytes 10616836 | tf_op jit(solution)/shard_map/while/body/eval_jaxpr/div | solution.py:61
  120.8 8.4 %multiply_reduce_fusion.2 = f32[4096]{0:T(1024)S(1)} fusion(f32[4,128,4096]{1,2,0:T(8,128)} %fusion.72, f32[128]{0:T(128)S(1)} %compare_convert_fusion.3, pred[128,4096]{0,1:T(8,128)(4,1)S(1)} %compare_and_fusion.2, bf16[128,4,128]{0,2,1:T(8,128)(2,1)S(1)} %bitcast.70, bf16[4096,1024]{1,0:T(8,128)(2,1)} %get-tuple-element.300, s32[]{:T(128)S(6)} %select_n.79), kind=kOutput, calls=%fused_computation.5.clone.1 | convolution fusion | flops 551551488 | bytes 10633732 | tf_op jit(solution)/shard_map/while/body/eval_jaxpr/sub | solution.py:59
  129.1 1.6 dynamic_update_slice.13
  130.7 1.3 compare_convert_fusion.3
  132.1 1.4 compare_and_fusion.2
  133.5 8.6 %fusion.72 = f32[4,128,4096]{1,2,0:T(8,128)} fusion(pred[128,4096]{0,1:T(8,128)(4,1)S(1)} %compare_and_fusion.2, bf16[128,4,128]{0,2,1:T(8,128)(2,1)S(1)} %bitcast.69, bf16[4096,1024]{1,0:T(8,128)(2,1)} %get-tuple-element.300, s32[]{:T(128)S(6)} %select_n.79), kind=kOutput, calls=%fused_computation.2.clone.1 | convolution fusion | flops 545268736 | bytes 10616836 | tf_op jit(solution)/shard_map/while/body/eval_jaxpr/div | solution.py:61
  142.1 8.4 %multiply_reduce_fusion.2 = f32[4096]{0:T(1024)S(1)} fusion(f32[4,128,4096]{1,2,0:T(8,128)} %fusion.72, f32[128]{0:T(128)S(1)} %compare_convert_fusion.3, pred[128,4096]{0,1:T(8,128)(4,1)S(1)} %compare_and_fusion.2, bf16[128,4,128]{0,2,1:T(8,128)(2,1)S(1)} %bitcast.70, bf16[4096,1024]{1,0:T(8,128)(2,1)} %get-tuple-element.300, s32[]{:T(128)S(6)} %select_n.79), kind=kOutput, calls=%fused_computation.5.clone.1 | convolution fusion | flops 551551488 | bytes 10633732 | tf_op jit(solution)/shard_map/while/body/eval_jaxpr/sub | solution.py:59
  150.5 1.6 dynamic_update_slice.13
  152.1 1.3 compare_convert_fusion.3
  153.4 1.4 compare_and_fusion.2
  154.8 8.6 %fusion.72 = f32[4,128,4096]{1,2,0:T(8,128)} fusion(pred[128,4096]{0,1:T(8,128)(4,1)S(1)} %compare_and_fusion.2, bf16[128,4,128]{0,2,1:T(8,128)(2,1)S(1)} %bitcast.69, bf16[4096,1024]{1,0:T(8,128)(2,1)} %get-tuple-element.300, s32[]{:T(128)S(6)} %select_n.79), kind=kOutput, calls=%fused_computation.2.clone.1 | convolution fusion | flops 545268736 | bytes 10616836 | tf_op jit(solution)/shard_map/while/body/eval_jaxpr/div | solution.py:61
  163.4 8.4 %multiply_reduce_fusion.2 = f32[4096]{0:T(1024)S(1)} fusion(f32[4,128,4096]{1,2,0:T(8,128)} %fusion.72, f32[128]{0:T(128)S(1)} %compare_convert_fusion.3, pred[128,4096]{0,1:T(8,128)(4,1)S(1)} %compare_and_fusion.2, bf16[128,4,128]{0,2,1:T(8,128)(2,1)S(1)} %bitcast.70, bf16[4096,1024]{1,0:T(8,128)(2,1)} %get-tuple-element.300, s32[]{:T(128)S(6)} %select_n.79), kind=kOutput, calls=%fused_computation.5.clone.1 | convolution fusion | flops 551551488 | bytes 10633732 | tf_op jit(solution)/shard_map/while/body/eval_jaxpr/sub | solution.py:59
  171.8 1.6 dynamic_update_slice.13
  173.4 1.3 compare_convert_fusion.3
  174.7 1.4 compare_and_fusion.2
  176.1 8.6 %fusion.72 = f32[4,128,4096]{1,2,0:T(8,128)} fusion(pred[128,4096]{0,1:T(8,128)(4,1)S(1)} %compare_and_fusion.2, bf16[128,4,128]{0,2,1:T(8,128)(2,1)S(1)} %bitcast.69, bf16[4096,1024]{1,0:T(8,128)(2,1)} %get-tuple-element.300, s32[]{:T(128)S(6)} %select_n.79), kind=kOutput, calls=%fused_computation.2.clone.1 | convolution fusion | flops 545268736 | bytes 10616836 | tf_op jit(solution)/shard_map/while/body/eval_jaxpr/div | solution.py:61
  184.7 8.4 %multiply_reduce_fusion.2 = f32[4096]{0:T(1024)S(1)} fusion(f32[4,128,4096]{1,2,0:T(8,128)} %fusion.72, f32[128]{0:T(128)S(1)} %compare_convert_fusion.3, pred[128,4096]{0,1:T(8,128)(4,1)S(1)} %compare_and_fusion.2, bf16[128,4,128]{0,2,1:T(8,128)(2,1)S(1)} %bitcast.70, bf16[4096,1024]{1,0:T(8,128)(2,1)} %get-tuple-element.300, s32[]{:T(128)S(6)} %select_n.79), kind=kOutput, calls=%fused_computation.5.clone.1 | convolution fusion | flops 551551488 | bytes 10633732 | tf_op jit(solution)/shard_map/while/body/eval_jaxpr/sub | solution.py:59
  193.1 1.6 dynamic_update_slice.13
  194.7 1.3 compare_convert_fusion.3
  196.0 1.4 compare_and_fusion.2
  197.4 8.6 %fusion.72 = f32[4,128,4096]{1,2,0:T(8,128)} fusion(pred[128,4096]{0,1:T(8,128)(4,1)S(1)} %compare_and_fusion.2, bf16[128,4,128]{0,2,1:T(8,128)(2,1)S(1)} %bitcast.69, bf16[4096,1024]{1,0:T(8,128)(2,1)} %get-tuple-element.300, s32[]{:T(128)S(6)} %select_n.79), kind=kOutput, calls=%fused_computation.2.clone.1 | convolution fusion | flops 545268736 | bytes 10616836 | tf_op jit(solution)/shard_map/while/body/eval_jaxpr/div | solution.py:61
  206.0 8.4 %multiply_reduce_fusion.2 = f32[4096]{0:T(1024)S(1)} fusion(f32[4,128,4096]{1,2,0:T(8,128)} %fusion.72, f32[128]{0:T(128)S(1)} %compare_convert_fusion.3, pred[128,4096]{0,1:T(8,128)(4,1)S(1)} %compare_and_fusion.2, bf16[128,4,128]{0,2,1:T(8,128)(2,1)S(1)} %bitcast.70, bf16[4096,1024]{1,0:T(8,128)(2,1)} %get-tuple-element.300, s32[]{:T(128)S(6)} %select_n.79), kind=kOutput, calls=%fused_computation.5.clone.1 | convolution fusion | flops 551551488 | bytes 10633732 | tf_op jit(solution)/shard_map/while/body/eval_jaxpr/sub | solution.py:59
  214.4 1.6 dynamic_update_slice.13
  216.0 1.3 compare_convert_fusion.3
  217.4 1.4 compare_and_fusion.2
  218.8 8.6 %fusion.72 = f32[4,128,4096]{1,2,0:T(8,128)} fusion(pred[128,4096]{0,1:T(8,128)(4,1)S(1)} %compare_and_fusion.2, bf16[128,4,128]{0,2,1:T(8,128)(2,1)S(1)} %bitcast.69, bf16[4096,1024]{1,0:T(8,128)(2,1)} %get-tuple-element.300, s32[]{:T(128)S(6)} %select_n.79), kind=kOutput, calls=%fused_computation.2.clone.1 | convolution fusion | flops 545268736 | bytes 10616836 | tf_op jit(solution)/shard_map/while/body/eval_jaxpr/div | solution.py:61
  227.4 8.4 %multiply_reduce_fusion.2 = f32[4096]{0:T(1024)S(1)} fusion(f32[4,128,4096]{1,2,0:T(8,128)} %fusion.72, f32[128]{0:T(128)S(1)} %compare_convert_fusion.3, pred[128,4096]{0,1:T(8,128)(4,1)S(1)} %compare_and_fusion.2, bf16[128,4,128]{0,2,1:T(8,128)(2,1)S(1)} %bitcast.70, bf16[4096,1024]{1,0:T(8,128)(2,1)} %get-tuple-element.300, s32[]{:T(128)S(6)} %select_n.79), kind=kOutput, calls=%fused_computation.5.clone.1 | convolution fusion | flops 551551488 | bytes 10633732 | tf_op jit(solution)/shard_map/while/body/eval_jaxpr/sub | solution.py:59
  235.7 1.6 dynamic_update_slice.13
  237.4 5.5 %all-to-all-start = ((f32[32,8,128]{2,1,0:T(8,128)}), f32[32,8,128]{2,1,0:T(8,128)S(1)}, u32[]{:S(2)}, u32[]{:S(2)}) async-start(f32[32,8,128]{2,1,0:T(8,128)} %bitcast.9), calls=%async_computation | async-start | bytes 262144 | tf_op jit(solution)/shard_map/all_to_all | solution.py:16
  243.1 6.5 %multiply_convert_fusion = (bf16[128,1024]{1,0:T(8,128)(2,1)S(1)}, f32[128,1024]{1,0:T(8,128)S(1)}) fusion(f32[1024]{0:T(1024)S(1)} %copy-done.1, bf16[6144,1024]{1,0:T(8,128)(2,1)} %param.16, bf16[128,1024]{0,1:T(8,128)(2,1)S(1)} %bitcast.73, bf16[128,1024]{0,1:T(8,128)(2,1)S(1)} %bitcast.71, bf16[128,4096]{0,1:T(8,128)(2,1)S(1)} %get-tuple-element.317), kind=kOutput, calls=%fused_computation.42 | convolution fusion | flops 1616117760 | bytes 14946304 | tf_op jit(solution)/shard_map/dot_general | solution.py:71
  249.6 0.7 compare_convert_fusion.1
  250.3 0.3 all-to-all-done
  250.6 0.3 convert_reduce_fusion.1
  250.9 0.4 convert_reduce_fusion
  251.3 13.2 %fusion.46 = f32[6144,1024]{1,0:T(8,128)} fusion(bf16[128,1024]{1,0:T(8,128)(2,1)S(1)} %get-tuple-element.212, bf16[128,1024]{0,1:T(8,128)(2,1)S(1)} %bitcast.74, bf16[128,1024]{0,1:T(8,128)(2,1)S(1)} %bitcast.72, bf16[128,4096]{0,1:T(8,128)(2,1)S(1)} %get-tuple-element.317), kind=kOutput, calls=%fused_computation.40 | convolution fusion | flops 1615331328 | bytes 27000832 | tf_op jit(solution)/shard_map/dot_general | solution.py:93
  264.5 0.3 fusion.52
  264.8 0.3 reshape.87
  265.0 66.5 %psum.7 = f32[9224]{0:T(1024)S(1)} all-reduce(f32[9224]{0:T(1024)S(1)} %pad_maximum_fusion.3), channel_id=1, replica_groups=mesh['seq'=32,'batch'=4] {'seq','batch'}, use_global_device_ids=true, to_apply=%region_9.10 | all-reduce | flops 9224 | bytes 73792 | tf_op jit(solution)/shard_map/psum | solution.py:24
  331.5 0.5 slice.22
  332.1 0.6 slice.20
  332.6 0.3 reshape.88
  332.9 0.8 copy.18
  333.7 176.9 %reduce-scatter.2.cloned.1.call-done = f32[48,1024]{1,0:T(8,128)} async-done(((f32[6144,1024]{1,0:T(8,128)}), f32[48,1024]{1,0:T(8,128)}) %reduce-scatter.2.cloned.1.call-update) | async-done | bytes 196624 | tf_op jit(solution)/shard_map/reduce_scatter | solution.py:92
  (23 shorter events, 0.6 us)
Async XLA Ops:
  7.2 243.4 %copy-start = (bf16[1024,8]{0,1:T(8,128)(2,1)S(1)}, bf16[1024,8]{0,1:T(8,128)(2,1)}, u32[]{:S(2)}) copy-start(bf16[1024,8]{0,1:T(8,128)(2,1)} %param.18) | copy-start | bytes 49156
  7.2 59.6 %all-gather.3.cloned.1.call-start = ((), (), s32[]{:S(2)}) async-start(), calls=%async_computation.3 | async-start | bytes 8650752 | tf_op jit(solution)/shard_map/all_gather | solution.py:37
  66.8 176.4 %copy-start.1 = (f32[1024]{0:T(1024)S(1)}, f32[1024]{0:T(1024)}, u32[]{:S(2)}) copy-start(f32[1024]{0:T(1024)} %param.17) | copy-start | bytes 12292
  237.4 13.2 %all-to-all-start = ((f32[32,8,128]{2,1,0:T(8,128)}), f32[32,8,128]{2,1,0:T(8,128)S(1)}, u32[]{:S(2)}, u32[]{:S(2)}) async-start(f32[32,8,128]{2,1,0:T(8,128)} %bitcast.9), calls=%async_computation | async-start | bytes 262144 | tf_op jit(solution)/shard_map/all_to_all | solution.py:16
  242.9 267.8 %reduce-scatter.2.cloned.1.call-start = ((), (), s32[]{:S(2)}) async-start(), calls=%async_computation.2 | async-start | bytes 25362432 | tf_op jit(solution)/shard_map/reduce_scatter | solution.py:92
  243.1 7.5 %copy-start.2 = (f32[8]{0:T(128)S(1)}, f32[8]{0:T(128)}, u32[]{:S(2)}) copy-start(f32[8]{0:T(128)} %param.19) | copy-start | bytes 100
Sparse Core Ops, SparseCore 0:
  10.3 56.4 all-gather.2
  264.6 245.9 reduce-scatter.1
where the time goes:
time: 520 us; the launch traced here: 518 us
  waiting for transfers between devices  229 us (44%)
  matrix products  156 us (30%)
  blocking collectives  66.5 us (13%)
  other arithmetic  24.9 us (5%)
  local copies, waits for them, and re-layouts  19.4 us (4%)
  between operations  14.8 us (3%)
  starting transfers between devices  5.78 us (1%)
    reduce_scatter x1, waiting for transfers between devices, on_device(): lax.psum_scatter(lax.dot_general(features, delta, (((0,), (0,)), ((), ())...  177 us
    div x8, matrix products, group_mass(): share = weights / denom * query_live[None, :, None]  68.8 us
    sub x8, matrix products, group_mass(): weights = jnp.where(allowed[None], jnp.exp(masked - top), 0.0)  67 us
    psum x1, blocking collectives, in_one(): so_far = lax.psum(jnp.concatenate([a.ravel() for a in arrays]), axis)  66.5 us
    all_gather x1, waiting for transfers between devices, on_device(): every_key = lax.all_gather(k_rows, 'seq', axis=0, tiled=True)  51.6 us
    dot_general x1, matrix products, on_device(): lax.dot_general(features, delta, (((0,), (0,)), ((), ())), preferred_elem...  13.2 us
    dynamic_update_slice x8, local copies, waits for them, and re-layouts, group_mass(): return lax.dynamic_update_index_in_dim(sums, column, index, 0)  12.9 us
    and x8, other arithmetic, on_device(): (key_pos[None, :] <= query_pos[:, None]) & (key_pos < limit)[None, :]  11.1 us
  transfers between devices with their start and end apart: 3, of which 3 were waited for; matrix products, arithmetic and copies ran while one was open for 3% of the time, Pallas kernels for 0%

commit v1 on v0

v1 whole, which is shorter than its diff:
```python
import functools, math
import jax, jax.numpy as jnp
from jax import lax
from jax.experimental import pallas as pl
from jax.experimental.pallas import tpu as pltpu
from jax.sharding import PartitionSpec as P

NEG = -1e30

def attn_body(tq, kc, sub, blocks, rows, scale2, order_ref, limit_ref, q_hbm, k_hbm, out_ref, qs, ks, s_ref, acc_ref, sems):
    total = blocks * rows
    def issue(s, _):
        p = order_ref[s]
        dst = pl.ds(pl.multiple_of(p * rows, rows), rows)
        pltpu.make_async_copy(q_hbm.at[s], qs.at[dst], sems.at[0]).start()
        pltpu.make_async_copy(k_hbm.at[s], ks.at[dst], sems.at[1]).start()
        return 0
    lax.fori_loop(0, blocks, issue, 0)
    acc_ref[...] = jnp.zeros_like(acc_ref)
    for src, dst, i in ((q_hbm, qs, 0), (k_hbm, ks, 1)):
        pltpu.make_async_copy(src, src, sems.at[i]).wait()
    limit = limit_ref[0]
    lanes = 128
    groups = tq // lanes

    def tile(i, _):
        q0 = pl.multiple_of(i * tq, tq)
        q_part = qs[pl.ds(q0, tq), :]

        def scores(r0, mx, masked):
            k_part = ks[pl.ds(r0, kc), :]
            s = lax.dot_general(k_part, q_part, (((1,), (1,)), ((), ())), preferred_element_type=jnp.float32)
            if masked:
                kp = r0 + lax.broadcasted_iota(jnp.int32, (kc, tq), 0)
                qp = q0 + lax.broadcasted_iota(jnp.int32, (kc, tq), 1)
                s = jnp.where(kp <= qp, s, NEG)
            s_ref[pl.ds(r0, kc), :] = s
            return jnp.maximum(mx, jnp.max(s.reshape(kc // 8, 8, tq), axis=0))

        n_full = i * (tq // kc)
        mx = lax.fori_loop(0, n_full, lambda j, m: scores(pl.multiple_of(j * kc, kc), m, False), jnp.full((8, tq), NEG, jnp.float32))
        for d in range(tq // kc):
            mx = scores(pl.multiple_of(q0 + d * kc, kc), mx, True)
        top = jnp.max(mx, axis=0, keepdims=True)
        top8 = jnp.broadcast_to(top, (8, tq))
        n_sub = (i + 1) * (tq // sub)

        def weights(j, l):
            r0 = pl.multiple_of(j * sub, sub)
            s = s_ref[pl.ds(r0, sub), :].reshape(sub // 8, 8, tq)
            w = jnp.exp2((s - top8[None]) * scale2)
            s_ref[pl.ds(r0, sub), :] = w.reshape(sub, tq)
            return l + jnp.sum(w, axis=0)

        l = lax.fori_loop(0, n_sub, weights, jnp.zeros((8, tq), jnp.float32))
        denom = jnp.sum(l, axis=0, keepdims=True)
        qpos = q0 + lax.broadcasted_iota(jnp.int32, (1, tq), 1)
        rec = jnp.where(qpos < limit, 1.0 / denom, 0.0)
        rec8 = jnp.broadcast_to(rec, (8, tq))

        def shares(j, _):
            r0 = pl.multiple_of(j * sub, sub)
            w = s_ref[pl.ds(r0, sub), :].reshape(sub // 8, 8, tq) * rec8[None]
            w = w.reshape(sub, tq)
            tot = w[:, :lanes]
            for g in range(1, groups):
                tot = tot + w[:, g * lanes:(g + 1) * lanes]
            acc_ref[pl.ds(r0, sub), :] += tot
            return 0
        lax.fori_loop(0, n_sub, shares, 0)
        return 0

    lax.fori_loop(0, total // tq, tile, 0)

    def emit(s, _):
        p = order_ref[s]
        part = acc_ref[pl.ds(pl.multiple_of(p * rows, rows), rows), :]
        out_ref[pl.ds(s, 1), :] = jnp.sum(part.T, axis=0, keepdims=True)
        return 0
    lax.fori_loop(0, blocks, emit, 0)


def attention(order, limit, q_all, k_all, tq=512, kc=128, sub=64):
    blocks, rows, head = q_all.shape
    total = blocks * rows
    scale2 = math.log2(math.e) / math.sqrt(head)
    return pl.pallas_call(
        functools.partial(attn_body, tq, kc, sub, blocks, rows, scale2),
        out_shape=jax.ShapeDtypeStruct((blocks, rows), jnp.float32),
        in_specs=[pl.BlockSpec(memory_space=pltpu.SMEM)] * 2 + [pl.BlockSpec(memory_space=pl.ANY)] * 2,
        out_specs=pl.BlockSpec(memory_space=pltpu.VMEM),
        scratch_shapes=[
            pltpu.VMEM((total, head), jnp.bfloat16),
            pltpu.VMEM((total, head), jnp.bfloat16),
            pltpu.VMEM((total, tq), jnp.float32),
            pltpu.VMEM((total, 128), jnp.float32),
            pltpu.SemaphoreType.DMA((2,)),
        ],
        compiler_params=pltpu.CompilerParams(vmem_limit_bytes=48 * 2**20),
        cost_estimate=pl.CostEstimate(flops=total * total * head, bytes_accessed=4 * total * head, transcendentals=total * total // 2),
        name="mass",
    )(order, limit, q_all, k_all)


def on_device(queries, keys, values, lengths, block_pos, w_in, b_in, output_weight, output_bias):
    q_rows, k_rows, v_rows = queries[0], keys[0], values[0]
    rows = q_rows.shape[0]
    heads_kv = output_weight.shape[1]
    head = k_rows.shape[1] // heads_kv
    n = lax.axis_size("seq")
    per = q_rows.shape[1] // k_rows.shape[1]
    total = n * rows
    mine = lax.axis_index("seq")
    q_send = q_rows.reshape(rows, n, head).transpose(1, 0, 2)
    k_send = jnp.repeat(k_rows.reshape(rows, heads_kv, head).transpose(1, 0, 2), per, axis=0)
    both = lax.all_to_all(jnp.concatenate([q_send, k_send], axis=2), "seq", 0, 0, tiled=True)
    mass_own = attention(block_pos[0], lengths, both[:, :, :head], both[:, :, head:], 512, 512, 64)
    features = jnp.concatenate([q_rows, k_rows, v_rows], axis=1)
    cols = features.shape[1] // n
    f_mine = lax.all_to_all(features.reshape(rows, n, cols).transpose(1, 0, 2), "seq", 0, 0, tiled=True).reshape(total, cols)
    pre = jnp.dot(features, w_in, preferred_element_type=jnp.float32) + b_in
    sig = jax.nn.sigmoid(pre)
    act = (pre * sig).astype(jnp.bfloat16)
    slope = sig * (1.0 + pre * (1.0 - sig))
    pred = jnp.dot(act, output_weight, preferred_element_type=jnp.float32) + output_bias
    offsets = jnp.arange(rows, dtype=jnp.int32)
    query_pos = lax.dynamic_index_in_dim(block_pos[0], mine, 0, keepdims=False) * rows + offsets
    query_live = (query_pos < lengths[0]).astype(jnp.float32)
    norm = 1.0 / math.sqrt(lax.axis_size("batch") * total)

    mass = lax.all_to_all(mass_own, "seq", 0, 0, tiled=True)
    mass = jnp.sum(mass.reshape(heads_kv, per, rows), axis=1)
    labels = jnp.log1p(mass).T
    resid = ((pred - labels) * query_live[:, None] * norm).astype(jnp.bfloat16)
    back = lax.dot_general(resid, output_weight, (((1,), (1,)), ((), ())), preferred_element_type=jnp.float32)
    delta = (back * slope).astype(jnp.bfloat16)
    every_delta = lax.all_gather(delta, "seq", axis=0, tiled=True)
    out_term = lax.dot_general(resid, act, (((0,), (0,)), ((), ())), preferred_element_type=jnp.float32)
    small = jnp.concatenate([
        jnp.sum(delta.astype(jnp.float32), axis=0),
        out_term.ravel(),
        jnp.sum(resid.astype(jnp.float32), axis=0)])
    small = lax.psum(small, ("seq", "batch"))
    h = b_in.shape[0]
    grad_b_in = small[:h]
    output_weight_gradient = small[h:h + h * heads_kv].reshape(heads_kv, h).T
    output_bias_gradient = small[h + h * heads_kv:]
    part = lax.dot_general(f_mine, every_delta, (((0,), (0,)), ((), ())), preferred_element_type=jnp.float32)
    grad_w_in = lax.psum_scatter(part, "batch", scatter_dimension=0, tiled=True)
    return (grad_w_in, grad_b_in, output_weight_gradient, output_bias_gradient)


def solution(mesh):
    return jax.shard_map(
        on_device,
        mesh=mesh,
        in_specs=(
            P("batch", "seq", None),
            P("batch", "seq", None),
            P("batch", "seq", None),
            P("batch"),
            P("batch", None),
            P(),
            P(),
            P(),
            P(),
        ),
        out_specs=(P(("seq", "batch"), None), P(), P(), P()),
        check_vma=False,
    )
```

time: 520 us -> 235 us (0.45)
  waiting for transfers between devices: 229 us -> 51.1 us
  matrix products: 156 us -> 15 us
  Pallas kernels: 0 us -> 31.7 us
  blocking collectives: 66.5 us -> 96 us
  other arithmetic: 24.9 us -> 2.97 us
  local copies, waits for them, and re-layouts: 19.4 us -> 8.85 us
  starting transfers between devices: 5.78 us -> 14.2 us
    reduce_scatter x1, waiting for transfers between devices: 177 us -> 0.01 us  [on_device(): grad_w_in = lax.psum_scatter(part, 'batch', scatter_dimension=0, tiled=True)]
    div x8 -> x0, matrix products: 68.8 us -> none  [group_mass(): share = weights / denom * query_live[None, :, None]]
    sub x8 -> x0, matrix products: 67 us -> none  [group_mass(): weights = jnp.where(allowed[None], jnp.exp(masked - top), 0.0)]
    pallas_call x0 -> x1, Pallas kernels: none -> 31.7 us  [attention(): pl.pallas_call(functools.partial(attn_body, tq, kc, sub, blocks, rows, sc...]
    all_to_all x0 -> x1, blocking collectives: none -> 30.8 us  [on_device(): lax.all_to_all(features.reshape(rows, n, cols).transpose(1, 0, 2), 'seq',...]
    all_gather x1, waiting for transfers between devices: 51.6 us -> 28 us  [on_device(): every_delta = lax.all_gather(delta, 'seq', axis=0, tiled=True)]
    all_to_all x1 -> x2, waiting for transfers between devices: 0.27 us -> 23 us  [the longest x1 16.7 us: on_device(): lax.all_to_all(jnp.concatenate([q_send, k_send], axis=2), 'seq', 0, 0, ti...]
    dynamic_update_slice x8 -> x0, local copies, waits for them, and re-layouts: 12.9 us -> none  [group_mass(): return lax.dynamic_update_index_in_dim(sums, column, index, 0)]
  transfers between devices with their start and end apart: 3 -> 4, of which waited for: 3 -> 3; matrix products, arithmetic and copies ran while one was open for 3% -> 6% of each run, Pallas kernels for 0% -> 0%
where the time goes in v1:
time: 235 us
  blocking collectives  96 us (41%)
  waiting for transfers between devices  51.1 us (22%)
  Pallas kernels  31.7 us (13%)
  matrix products  15 us (6%)
  between operations  14.9 us (6%)
  starting transfers between devices  14.2 us (6%)
  local copies, waits for them, and re-layouts  8.85 us (4%)
  other arithmetic  2.97 us (1%)
    psum x1, blocking collectives, on_device(): small = lax.psum(small, ('seq', 'batch'))  65.2 us
    pallas_call x1, Pallas kernels, attention(): pl.pallas_call(functools.partial(attn_body, tq, kc, sub, blocks, rows, sc...  31.7 us
    all_to_all x1, blocking collectives, on_device(): lax.all_to_all(features.reshape(rows, n, cols).transpose(1, 0, 2), 'seq',...  30.8 us
    all_gather x1, waiting for transfers between devices, on_device(): every_delta = lax.all_gather(delta, 'seq', axis=0, tiled=True)  28 us
    all_to_all x1, waiting for transfers between devices, on_device(): lax.all_to_all(jnp.concatenate([q_send, k_send], axis=2), 'seq', 0, 0, ti...  16.7 us
    all_to_all x1, starting transfers between devices, on_device(): lax.all_to_all(jnp.concatenate([q_send, k_send], axis=2), 'seq', 0, 0, ti...  9.72 us
    dot_general x1, matrix products, on_device(): pre = jnp.dot(features, w_in, preferred_element_type=jnp.float32) + b_in  7.4 us
    all_to_all x1, waiting for transfers between devices, on_device(): mass = lax.all_to_all(mass_own, 'seq', 0, 0, tiled=True)  6.3 us
  transfers between devices with their start and end apart: 4, of which 3 were waited for; matrix products, arithmetic and copies ran while one was open for 6% of the time, Pallas kernels for 0%

profile of v1, /device:TPU:1, one launch (start us, length us, event | category | flops | bytes accessed | tf_op | source)
XLA Modules:
  0.0 234.7 jit_solution(7554417735107459039)
XLA Ops:
  7.2 0.0 copy-start
  7.2 1.0 copy.30
  8.2 1.6 copy.21
  9.9 0.7 copy.26
  10.5 0.2 broadcast_in_dim.2
  10.8 1.6 pad_maximum_fusion
  12.4 0.0 copy-start.1
  12.4 0.0 copy-start.4
  12.4 9.7 %all-to-all-start.1 = ((bf16[32,128,256]{2,1,0:T(8,128)(2,1)}), bf16[32,128,256]{2,1,0:T(8,128)(2,1)S(1)}, u32[]{:S(2)}, u32[]{:S(2)}) async-start(bf16[32,128,256]{2,1,0:T(8,128)(2,1)} %pad_maximum_fusion), calls=%async_computation.1 | async-start | bytes 4194304 | tf_op jit(solution)/shard_map/all_to_all | solution.py:116
  22.1 1.1 copy.22
  23.9 1.8 copy.23
  25.7 0.0 copy-done.1
  25.7 0.6 fusion.9
  26.3 0.0 copy-done.4
  26.3 7.4 %multiply_convert_fusion = (bf16[128,1024]{1,0:T(8,128)(2,1)}, f32[128,1024]{1,0:T(8,128)}) fusion(f32[1024]{0:T(1024)S(1)} %copy-done.4, bf16[6144,1024]{1,0:T(8,128)(2,1)} %param.14, bf16[128,1024]{0,1:T(8,128)(2,1)} %bitcast.54, bf16[128,1024]{0,1:T(8,128)(2,1)S(1)} %bitcast.52, bf16[128,4096]{0,1:T(8,128)(2,1)S(1)} %bitcast.47), kind=kOutput, calls=%fused_computation.15 | convolution fusion | flops 1616117760 | bytes 14946304 | tf_op jit(solution)/shard_map/dot_general | solution.py:121
  33.7 16.7 %all-to-all-done.1 = bf16[32,128,256]{2,1,0:T(8,128)(2,1)S(1)} async-done(((bf16[32,128,256]{2,1,0:T(8,128)(2,1)}), bf16[32,128,256]{2,1,0:T(8,128)(2,1)S(1)}, u32[]{:S(2)}, u32[]{:S(2)}) %all-to-all-start.1) | async-done | bytes 2097184 | tf_op jit(solution)/shard_map/all_to_all | solution.py:116
  50.4 0.6 fusion.8
  51.0 0.0 copy-start.3
  51.1 0.0 copy-start.5
  51.1 0.0 copy-start.6
  51.1 31.7 %mass.1 = f32[32,128]{1,0:T(8,128)} custom-call(s32[32]{0:T(128)S(1)} %bitcast.45, s32[1]{0:T(128)} %copy.38.limit_ref, bf16[32,128,128]{2,1,0:T(8,128)(2,1)S(1)} %get-tuple-element.5.q_hbm, bf16[32,128,128]{2,1,0:T(8,128)(2,1)S(1)} %get-tuple-element.4.k_hbm), custom_call_target="tpu_custom_call" | custom-call | flops 2147483648 | bytes 2097152 | tf_op jit(solution)/shard_map/mass/pallas_call | solution.py:87
  82.8 0.0 copy-start.2
  82.8 4.4 %all-to-all-start.2 = ((f32[32,1,128]{2,1,0:T(1,128)}), f32[32,1,128]{2,1,0:T(1,128)S(1)}, u32[]{:S(2)}, u32[]{:S(2)}) async-start(f32[32,1,128]{2,1,0:T(1,128)} %bitcast.11), calls=%async_computation.2 | async-start | bytes 32768 | tf_op jit(solution)/shard_map/all_to_all | solution.py:131
  87.2 0.0 all-gather.2.cloned.1.call-start
  87.3 0.7 compare_convert_fusion
  88.0 6.3 %all-to-all-done.2 = f32[32,1,128]{2,1,0:T(1,128)S(1)} async-done(((f32[32,1,128]{2,1,0:T(1,128)}), f32[32,1,128]{2,1,0:T(1,128)S(1)}, u32[]{:S(2)}, u32[]{:S(2)}) %all-to-all-start.2) | async-done | bytes 16416 | tf_op jit(solution)/shard_map/all_to_all | solution.py:131
  94.3 0.0 copy-done
  94.3 0.0 copy-done.3
  94.3 0.0 copy-done.5
  94.3 0.3 convert_reduce_fusion.1
  94.6 0.0 copy-done.6
  94.6 1.1 convert_reduce_fusion
  95.7 0.0 all-gather.2.cloned.1.call-update
  95.7 0.0 reduce-scatter.2.cloned.1.call-start
  95.7 0.0 copy-done.2
  95.8 0.1 pad_maximum_fusion.1
  95.9 30.8 %all_to_all.19 = bf16[32,128,192]{1,2,0:T(8,128)(2,1)S(1)} all-to-all(bf16[32,128,192]{1,2,0:T(8,128)(2,1)S(1)} %bitcast.49), channel_id=1, replica_groups=mesh['seq'=32,'batch'=4] {'seq'}, dimensions={0} | all-to-all | bytes 3145728 | tf_op jit(solution)/shard_map/all_to_all | solution.py:120
  126.6 28.0 %all-gather.2.cloned.1.call-done = bf16[4096,1024]{1,0:T(8,128)(2,1)} async-done(((bf16[128,1024]{1,0:T(8,128)(2,1)}), bf16[4096,1024]{1,0:T(8,128)(2,1)}) %all-gather.2.cloned.1.call-update) | async-done | bytes 8388624 | tf_op jit(solution)/shard_map/all_gather | solution.py:137
  154.6 6.1 %fusion = f32[192,1024]{1,0:T(8,128)} fusion(bf16[4096,1024]{1,0:T(8,128)(2,1)} %all-gather.2.cloned.1.call-done, bf16[32,128,192]{1,2,0:T(8,128)(2,1)S(1)} %all_to_all.19), kind=kOutput, calls=%fused_computation.1 | convolution fusion | flops 1610612736 | bytes 10747904 | tf_op jit(solution)/shard_map/dot_general | solution.py:148
  160.7 0.0 reduce-scatter.2.cloned.1.call-update
  160.8 0.1 convolution_bitcast_fusion
  160.9 65.2 %psum.7 = f32[9224]{0:T(1024)S(1)} all-reduce(f32[9224]{0:T(1024)S(1)} %pad_maximum_fusion.2), channel_id=1, replica_groups=mesh['seq'=32,'batch'=4] {'seq','batch'}, use_global_device_ids=true, to_apply=%region_4.5 | all-reduce | flops 9224 | bytes 73792 | tf_op jit(solution)/shard_map/psum | solution.py:143
  226.2 0.5 slice.24
  226.7 0.6 slice.22
  227.3 0.6 reshape.46
  227.9 0.0 reduce-scatter.2.cloned.1.call-done
  (5 shorter events, 0.1 us)
Async XLA Ops:
  7.2 87.1 %copy-start = (bf16[1024,8]{0,1:T(8,128)(2,1)S(1)}, bf16[1024,8]{0,1:T(8,128)(2,1)}, u32[]{:S(2)}) copy-start(bf16[1024,8]{0,1:T(8,128)(2,1)} %param.16) | copy-start | bytes 49156
  12.4 13.3 %copy-start.1 = (s32[1,32]{1,0:T(1,128)S(1)}, s32[1,32]{1,0:T(1,128)}, u32[]{:S(2)}) copy-start(s32[1,32]{1,0:T(1,128)} %param.13) | copy-start | bytes 388
  12.4 13.9 %copy-start.4 = (f32[1024]{0:T(1024)S(1)}, f32[1024]{0:T(1024)}, u32[]{:S(2)}) copy-start(f32[1024]{0:T(1024)} %param.15) | copy-start | bytes 12292
  12.4 38.1 %all-to-all-start.1 = ((bf16[32,128,256]{2,1,0:T(8,128)(2,1)}), bf16[32,128,256]{2,1,0:T(8,128)(2,1)S(1)}, u32[]{:S(2)}, u32[]{:S(2)}) async-start(bf16[32,128,256]{2,1,0:T(8,128)(2,1)} %pad_maximum_fusion), calls=%async_computation.1 | async-start | bytes 4194304 | tf_op jit(solution)/shard_map/all_to_all | solution.py:116
  51.0 43.2 %copy-start.3 = (bf16[128,1024]{1,0:T(8,128)(2,1)S(1)}, bf16[128,1024]{1,0:T(8,128)(2,1)}, u32[]{:S(2)}) copy-start(bf16[128,1024]{1,0:T(8,128)(2,1)} %get-tuple-element.6) | copy-start | bytes 786436
  51.1 43.2 %copy-start.5 = (f32[8]{0:T(128)S(1)}, f32[8]{0:T(128)}, u32[]{:S(2)}) copy-start(f32[8]{0:T(128)} %param.17) | copy-start | bytes 100
  51.1 43.5 %copy-start.6 = (f32[128,1024]{1,0:T(8,128)S(1)}, f32[128,1024]{1,0:T(8,128)}, u32[]{:S(2)}) copy-start(f32[128,1024]{1,0:T(8,128)} %get-tuple-element.7) | copy-start | bytes 1572868
  82.8 12.9 %copy-start.2 = (bf16[1,128,1024]{1,2,0:T(8,128)(2,1)S(1)}, bf16[1,128,1024]{1,2,0:T(8,128)(2,1)}, u32[]{:S(2)}) copy-start(bf16[1,128,1024]{1,2,0:T(8,128)(2,1)} %copy.23) | copy-start | bytes 786436
  82.8 11.4 %all-to-all-start.2 = ((f32[32,1,128]{2,1,0:T(1,128)}), f32[32,1,128]{2,1,0:T(1,128)S(1)}, u32[]{:S(2)}, u32[]{:S(2)}) async-start(f32[32,1,128]{2,1,0:T(1,128)} %bitcast.11), calls=%async_computation.2 | async-start | bytes 32768 | tf_op jit(solution)/shard_map/all_to_all | solution.py:131
  87.2 67.4 %all-gather.2.cloned.1.call-start = ((), (), s32[]{:S(2)}) async-start(), calls=%async_computation.4 | async-start | bytes 8650752 | tf_op jit(solution)/shard_map/all_gather | solution.py:137
  95.7 132.2 %reduce-scatter.2.cloned.1.call-start = ((), (), s32[]{:S(2)}) async-start(), calls=%async_computation.5 | async-start | bytes 983040 | tf_op jit(solution)/shard_map/reduce_scatter | solution.py:149
Sparse Core Ops, SparseCore 0:
  95.8 58.7 all-gather.1
  160.9 20.3 reduce-scatter.1

commit v2 on v1

--- a/solution.py
+++ b/solution.py
@@ -75,7 +75,7 @@
     def emit(s, _):
         p = order_ref[s]
         part = acc_ref[pl.ds(pl.multiple_of(p * rows, rows), rows), :]
-        out_ref[pl.ds(s, 1), :] = jnp.sum(part.T, axis=0, keepdims=True)
+        out_ref[s] = jnp.sum(part.T, axis=0, keepdims=True)
         return 0
     lax.fori_loop(0, blocks, emit, 0)
 
@@ -86,7 +86,7 @@
     scale2 = math.log2(math.e) / math.sqrt(head)
     return pl.pallas_call(
         functools.partial(attn_body, tq, kc, sub, blocks, rows, scale2),
-        out_shape=jax.ShapeDtypeStruct((blocks, rows), jnp.float32),
+        out_shape=jax.ShapeDtypeStruct((blocks, 1, rows), jnp.float32),
         in_specs=[pl.BlockSpec(memory_space=pltpu.SMEM)] * 2 + [pl.BlockSpec(memory_space=pl.ANY)] * 2,
         out_specs=pl.BlockSpec(memory_space=pltpu.VMEM),
         scratch_shapes=[
@@ -102,10 +102,354 @@
     )(order, limit, q_all, k_all)
 
 
-def on_device(queries, keys, values, lengths, block_pos, w_in, b_in, output_weight, output_bias):
+MESH = pl.DeviceIdType.MESH
+
+
+def remote(src, dst, send_sem, recv_sem, device):
+    return pltpu.make_async_remote_copy(
+        src_ref=src, dst_ref=dst, send_sem=send_sem, recv_sem=recv_sem, device_id=device, device_id_type=MESH
+    )
+
+
+def tail_body(dims, norm, mass_ref, pred_ref, live_ref, w2t_ref, slope_ref, act_ref, f_ref, grad_ref, small_ref,
+              mrecv, lab, dl, ft, part, pair, xrecv, sm, smr, zs, ys, xs,
+              m_send, m_recv, g_send, g_recv, p_send, p_recv, x_send, x_recv, s_send, s_recv):
+    ny, nz, nb = dims
+    n = ny * nz * 2
+    s, b = lax.axis_index("seq"), lax.axis_index("batch")
+    core, c = lax.rem(s, 2), s // 2
+    z, y = lax.rem(c, nz), c // nz
+    rows, hidden = slope_ref.shape
+    chunks, tokens, width = dl.shape
+    feats = part.shape[1]
+    half = feats // 2
+    own_rows = half // nb
+    partner = (s + 1 - 2 * core, b)
+
+    barrier = pltpu.get_barrier_semaphore()
+
+    def greet(r, _):
+        pl.semaphore_signal(barrier, inc=1, device_id=(lax.rem(s + r, n), b), device_id_type=MESH)
+        return 0
+    lax.fori_loop(1, n, greet, 0)
+    for r in range(1, nb):
+        pl.semaphore_signal(barrier, inc=1, device_id=(s, lax.rem(b + r, nb)), device_id_type=MESH)
+    pl.semaphore_wait(barrier, n - 1 + nb - 1)
+
+    def mass_copy(r, sender):
+        to = lax.rem(s + r, n)
+        return remote(mass_ref.at[to], mrecv.at[s], m_send.at[r], m_recv.at[s], (to, b))
+
+    def mass_start(r, _):
+        mass_copy(r, s).start()
+        return 0
+    lax.fori_loop(1, n, mass_start, 0)
+    mrecv[s] = mass_ref[s]
+
+    for k in range(tokens // rows):
+        ft[:, k * rows:(k + 1) * rows] = f_ref[k * rows:(k + 1) * rows, :].T
+
+    def mass_wait(r, _):
+        frm = lax.rem(s + n - r, n)
+        got = remote(mass_ref.at[frm], mrecv.at[frm], m_send.at[r], m_recv.at[frm], (frm, b))
+        got.wait_recv()
+        return 0
+    lax.fori_loop(1, n, mass_wait, 0)
+
+    heads = lab.shape[0]
+    per = n // heads
+    for g in range(heads):
+        total = mrecv[per * g]
+        for i in range(1, per):
+            total = total + mrecv[per * g + i]
+        lab[g:g + 1, :] = jnp.log1p(total)
+    resid_t = ((pred_ref[...] - lab[...]) * live_ref[...] * norm).astype(jnp.bfloat16)
+    resid = resid_t.astype(jnp.float32).T.astype(jnp.bfloat16)
+    back = jnp.dot(resid, w2t_ref[...], preferred_element_type=jnp.float32)
+    delta = (back * slope_ref[...]).astype(jnp.bfloat16)
+    here = pl.ds(pl.multiple_of(c * rows, rows), rows)
+    for j in range(chunks):
+        dl[j, here, :] = delta[:, j * width:(j + 1) * width]
+
+    wide = rows // 2
+    slot = {}
+
+    def number(*key):
+        return slot.setdefault(key, len(slot))
+
+    def spot(half_id, a, e):
+        return (a * nz + e) if half_id == 0 else (e * nz + a)
+
+    def ring(v, d, size):
+        return lax.rem(v + (d + size), size)
+
+    def coords(half_id):
+        return (y, z, ny, nz) if half_id == 0 else (z, y, nz, ny)
+
+    def piece(j, block, half_id, quarter):
+        r0 = half_id * wide + (quarter * (wide // 2) if quarter is not None else 0)
+        size = wide // 2 if quarter is not None else wide
+        return dl.at[j, pl.ds(pl.multiple_of(block * rows + r0, wide // 2), size), :]
+
+    def neighbour(half_id, which, d):
+        along_y = (half_id == 0) == (which == 0)
+        to_y = ring(y, d, ny) if along_y else y
+        to_z = z if along_y else ring(z, d, nz)
+        return ((to_y * nz + to_z) * 2 + core, b)
+
+    started = []
+
+    def copy(j, half_id, which, da, de, quarter, d):
+        a, e, na, ne = coords(half_id)
+        block = spot(half_id, ring(a, da, na), ring(e, de, ne))
+        ref = piece(j, block, half_id, quarter)
+        m = number(j, half_id, which, da, de, quarter, d)
+        return remote(ref, ref, g_send.at[m], g_recv.at[m], neighbour(half_id, which, d))
+
+    def send(j, half_id, which, da, de, quarter, d):
+        one = copy(j, half_id, which, da, de, quarter, d)
+        one.start()
+        started.append(one)
+
+    def receive(j, half_id, which, da, de, quarter, d):
+        a, e, na, ne = coords(half_id)
+        back_a, back_e = (da - d, de) if which == 0 else (da, de - d)
+        block = spot(half_id, ring(a, back_a, na), ring(e, back_e, ne))
+        ref = piece(j, block, half_id, quarter)
+        m = number(j, half_id, which, da, de, quarter, d)
+        remote(ref, ref, g_send.at[m], g_recv.at[m], neighbour(half_id, which, -d)).wait_recv()
+
+    def second(j, h, da):
+        for d in (1, -1):
+            send(j, h, 1, da, 0, None, d)
+
+    def second_pass_on(j, h, da):
+        receive(j, h, 1, da, 0, None, 1)
+        send(j, h, 1, da, -1, 0, 1)
+        receive(j, h, 1, da, 0, None, -1)
+        send(j, h, 1, da, 1, 1, -1)
+
+    def second_end(j, h, da):
+        receive(j, h, 1, da, -1, 0, 1)
+        receive(j, h, 1, da, 1, 1, -1)
+
+    def stage0(j):
+        for h in (0, 1):
+            for d in (1, -1):
+                send(j, h, 0, 0, 0, None, d)
+        for h in (0, 1):
+            second(j, h, 0)
+
+    def stage1(j):
+        for h in (0, 1):
+            receive(j, h, 0, 0, 0, None, 1)
+            send(j, h, 0, -1, 0, 0, 1)
+            second(j, h, -1)
+            receive(j, h, 0, 0, 0, None, -1)
+            send(j, h, 0, 1, 0, 1, -1)
+            second(j, h, 1)
+
+    def stage2(j):
+        for h in (0, 1):
+            second_pass_on(j, h, 0)
+        for h in (0, 1):
+            receive(j, h, 0, -1, 0, 0, 1)
+            receive(j, h, 0, 1, 0, 1, -1)
+            second(j, h, 2)
+
+    def stage3(j):
+        for da in (-1, 1):
+            for h in (0, 1):
+                second_pass_on(j, h, da)
+
+    def stage4(j):
+        for h in (0, 1):
+            second_pass_on(j, h, 2)
+
+    def stage5(j):
+        for da in (0, -1, 1, 2):
+            for h in (0, 1):
+                second_end(j, h, da)
+
+    def multiply(j):
+        part[j] = jnp.dot(ft[...], dl[j], preferred_element_type=jnp.float32)
+
+    def pair_copy(j, of):
+        ref = part.at[j, pl.ds(pl.multiple_of((1 - of) * half, half), half), :]
+        return remote(ref, pair.at[j], p_send.at[j], p_recv.at[j], partner)
+
+    def pair_start(j):
+        one = pair_copy(j, core)
+        one.start()
+        started.append(one)
+
+    def x_copy(j, r):
+        to = lax.rem(b + r, nb)
+        ref = pair.at[j, pl.ds(pl.multiple_of(to * own_rows, own_rows), own_rows), :]
+        return remote(ref, xrecv.at[j, r - 1], x_send.at[j, r - 1], x_recv.at[j, r - 1], (s, to))
+
+    def x_start(j):
+        pair_copy(j, core).wait_recv()
+        pair[j] = pair[j] + part[j, pl.ds(pl.multiple_of(core * half, half), half), :]
+        for r in (2, 1, 3)[: nb - 1]:
+            one = x_copy(j, r)
+            one.start()
+            started.append(one)
+
+    def x_end(j):
+        for r in range(1, nb):
+            x_copy(j, r).wait_recv()
+        own = pair[j, pl.ds(pl.multiple_of(b * own_rows, own_rows), own_rows), :]
+        for r in range(1, nb):
+            own = own + xrecv[j, r - 1]
+        grad_ref[:, j * width:(j + 1) * width] = own
+
+    def small_start0():
+        sw = sm.shape[2]
+        out_term = jnp.dot(resid_t, act_ref[...], preferred_element_type=jnp.float32)
+        sums = jnp.sum(delta.astype(jnp.float32), axis=0, keepdims=True)
+        bias = jnp.sum(resid_t.astype(jnp.float32), axis=1, keepdims=True)
+        lanes = 128
+        cols = [out_term[:, k * lanes:(k + 1) * lanes] for k in range(hidden // lanes)]
+        cols.append(jnp.concatenate([sums[:, k * lanes:(k + 1) * lanes] for k in range(hidden // lanes)], axis=0))
+        cols.append(jnp.broadcast_to(bias, (heads, lanes)))
+        each = sw // lanes
+        for k, value in enumerate(cols):
+            sm[k // each, :, (k % each) * lanes:(k % each + 1) * lanes] = value
+        one = remote(sm.at[1 - core], smr, s_send.at[0], s_recv.at[0], partner)
+        one.start()
+        started.append(one)
+
+    def small_hop(level, value, buf, at, size, target):
+        buf[at] = value
+        for r in range(1, size):
+            one = remote(buf.at[at], buf.at[at], s_send.at[level * 3 + r], s_recv.at[level * 3 + r], target(r))
+            one.start()
+            started.append(one)
+
+    def small_sum(level, buf, at, size, target):
+        for r in range(1, size):
+            frm = lax.rem(at + size - r, size)
+            remote(buf.at[frm], buf.at[frm], s_send.at[level * 3 + r], s_recv.at[level * 3 + r], target(r)).wait_recv()
+        total = buf[0]
+        for k in range(1, size):
+            total = total + buf[k]
+        return total
+
+    to_z = lambda r: ((y * nz + lax.rem(z + r, nz)) * 2 + core, b)
+    to_y = lambda r: ((lax.rem(y + r, ny) * nz + z) * 2 + core, b)
+    to_x = lambda r: (s, lax.rem(b + r, nb))
+
+    def small1():
+        remote(sm.at[1 - core], smr, s_send.at[0], s_recv.at[0], partner).wait_recv()
+        small_hop(0, sm[core] + smr[...], zs, z, nz, to_z)
+
+    def small2():
+        small_hop(1, small_sum(0, zs, z, nz, to_z), ys, y, ny, to_y)
+
+    def small3():
+        small_hop(2, small_sum(1, ys, y, ny, to_y), xs, b, nb, to_x)
+
+    def small4():
+        sm[core] = small_sum(2, xs, b, nb, to_x)
+        one = remote(sm.at[core], small_ref.at[core], s_send.at[10], s_recv.at[10], partner)
+        one.start()
+        started.append(one)
+        small_ref[core] = sm[core]
+
+    def small5():
+        remote(sm.at[1 - core], small_ref.at[1 - core], s_send.at[10], s_recv.at[10], partner).wait_recv()
+
+    if chunks == 2:
+        stage0(0); small_start0(); stage1(0); stage2(0); stage0(1); stage3(0); small1(); stage1(1); stage4(0)
+        stage2(1); stage5(0); small2(); stage3(1)
+        multiply(0); pair_start(0); stage4(1); small3()
+        x_start(0); stage5(1)
+        multiply(1); pair_start(1); small4(); x_end(0); x_start(1); small5(); x_end(1)
+    else:
+        small = [small1, small2, small3, small4, small5]
+        stage0(0); small_start0(); stage1(0); stage2(0)
+        for j in range(chunks):
+            last = j + 1 == chunks
+            if not last:
+                stage0(j + 1)
+            stage3(j)
+            if not last:
+                stage1(j + 1)
+            stage4(j)
+            if not last:
+                stage2(j + 1)
+            stage5(j)
+            if small:
+                small.pop(0)()
+            multiply(j)
+            pair_start(j)
+            if small:
+                small.pop(0)()
+            if j > 0:
+                x_end(j - 1)
+            x_start(j)
+        for one in small:
+            one()
+        x_end(chunks - 1)
+
+    for one in started:
+        one.wait_send()
+
+    def mass_drain(r, _):
+        mass_copy(r, s).wait_send()
+        return 0
+    lax.fori_loop(1, n, mass_drain, 0)
+
+
+def tail(dims, norm, mass, pred_t, live, w2t, slope, act, f, chunks=2):
+    ny, nz, nb = dims
+    n = mass.shape[0]
+    rows, hidden = slope.shape
+    tokens, feats = f.shape
+    heads = pred_t.shape[0]
+    width = hidden // chunks
+    half = feats // 2
+    sw = (hidden + 256) // 2
+    vm = pltpu.VMEM
+    dma = pltpu.SemaphoreType.DMA
+    return pl.pallas_call(
+        functools.partial(tail_body, dims, norm),
+        out_shape=(
+            jax.ShapeDtypeStruct((half // nb, hidden), jnp.float32),
+            jax.ShapeDtypeStruct((2, heads, sw), jnp.float32),
+        ),
+        in_specs=[pl.BlockSpec(memory_space=vm)] * 7,
+        out_specs=[pl.BlockSpec(memory_space=vm)] * 2,
+        scratch_shapes=[
+            vm((n, 1, rows), jnp.float32),
+            vm((heads, rows), jnp.float32),
+            vm((chunks, tokens, width), jnp.bfloat16),
+            vm((feats, tokens), jnp.bfloat16),
+            vm((chunks, feats, width), jnp.float32),
+            vm((chunks, half, width), jnp.float32),
+            vm((chunks, nb - 1, half // nb, width), jnp.float32),
+            vm((2, heads, sw), jnp.float32),
+            vm((heads, sw), jnp.float32),
+            vm((nz, heads, sw), jnp.float32),
+            vm((ny, heads, sw), jnp.float32),
+            vm((nb, heads, sw), jnp.float32),
+            dma((n,)), dma((n,)),
+            dma((chunks * 40,)), dma((chunks * 40,)),
+            dma((chunks,)), dma((chunks,)),
+            dma((chunks, nb - 1)), dma((chunks, nb - 1)),
+            dma((12,)), dma((12,)),
+        ],
+        compiler_params=pltpu.CompilerParams(collective_id=3, has_side_effects=True, vmem_limit_bytes=56 * 2**20),
+        cost_estimate=pl.CostEstimate(flops=2 * tokens * feats * hidden, bytes_accessed=8 * 2**20, transcendentals=0),
+        name="tail",
+    )(mass, pred_t, live, w2t, slope, act, f)
+
+
+def on_device(dims, queries, keys, values, lengths, block_pos, w_in, b_in, output_weight, output_bias):
     q_rows, k_rows, v_rows = queries[0], keys[0], values[0]
     rows = q_rows.shape[0]
-    heads_kv = output_weight.shape[1]
+    hidden, heads_kv = output_weight.shape
     head = k_rows.shape[1] // heads_kv
     n = lax.axis_size("seq")
     per = q_rows.shape[1] // k_rows.shape[1]
@@ -116,8 +460,12 @@
     both = lax.all_to_all(jnp.concatenate([q_send, k_send], axis=2), "seq", 0, 0, tiled=True)
     mass_own = attention(block_pos[0], lengths, both[:, :, :head], both[:, :, head:], 512, 512, 64)
     features = jnp.concatenate([q_rows, k_rows, v_rows], axis=1)
-    cols = features.shape[1] // n
-    f_mine = lax.all_to_all(features.reshape(rows, n, cols).transpose(1, 0, 2), "seq", 0, 0, tiled=True).reshape(total, cols)
+    chips = n // 2
+    cols = features.shape[1] // chips
+    planes = [[2 * i + core for i in range(chips)] for core in range(2)]
+    f_mine = lax.all_to_all(
+        features.reshape(rows, chips, cols).transpose(1, 0, 2), "seq", 0, 0, tiled=True, axis_index_groups=planes
+    ).reshape(chips * rows, cols)
     pre = jnp.dot(features, w_in, preferred_element_type=jnp.float32) + b_in
     sig = jax.nn.sigmoid(pre)
     act = (pre * sig).astype(jnp.bfloat16)
@@ -127,32 +475,17 @@
     query_pos = lax.dynamic_index_in_dim(block_pos[0], mine, 0, keepdims=False) * rows + offsets
     query_live = (query_pos < lengths[0]).astype(jnp.float32)
     norm = 1.0 / math.sqrt(lax.axis_size("batch") * total)
-
-    mass = lax.all_to_all(mass_own, "seq", 0, 0, tiled=True)
-    mass = jnp.sum(mass.reshape(heads_kv, per, rows), axis=1)
-    labels = jnp.log1p(mass).T
-    resid = ((pred - labels) * query_live[:, None] * norm).astype(jnp.bfloat16)
-    back = lax.dot_general(resid, output_weight, (((1,), (1,)), ((), ())), preferred_element_type=jnp.float32)
-    delta = (back * slope).astype(jnp.bfloat16)
-    every_delta = lax.all_gather(delta, "seq", axis=0, tiled=True)
-    out_term = lax.dot_general(resid, act, (((0,), (0,)), ((), ())), preferred_element_type=jnp.float32)
-    small = jnp.concatenate([
-        jnp.sum(delta.astype(jnp.float32), axis=0),
-        out_term.ravel(),
-        jnp.sum(resid.astype(jnp.float32), axis=0)])
-    small = lax.psum(small, ("seq", "batch"))
-    h = b_in.shape[0]
-    grad_b_in = small[:h]
-    output_weight_gradient = small[h:h + h * heads_kv].reshape(heads_kv, h).T
-    output_bias_gradient = small[h + h * heads_kv:]
-    part = lax.dot_general(f_mine, every_delta, (((0,), (0,)), ((), ())), preferred_element_type=jnp.float32)
-    grad_w_in = lax.psum_scatter(part, "batch", scatter_dimension=0, tiled=True)
-    return (grad_w_in, grad_b_in, output_weight_gradient, output_bias_gradient)
+    grad_w_in, small = tail(dims, norm, mass_own, pred.T, query_live[None, :], output_weight.T, slope, act, f_mine)
+    small = jnp.concatenate([small[0], small[1]], axis=1)
+    grad_b_in = small[:, hidden:hidden + 128].reshape(hidden)
+    return (grad_w_in, grad_b_in, small[:, :hidden].T, small[:, hidden + 128])
 
 
 def solution(mesh):
+    nb = mesh.shape["batch"]
+    ny = nz = math.isqrt(mesh.shape["seq"] // 2)
     return jax.shard_map(
-        on_device,
+        functools.partial(on_device, (ny, nz, nb)),
         mesh=mesh,
         in_specs=(
             P("batch", "seq", None),

time: 235 us -> 149 us (0.63)
  blocking collectives: 96 us -> 0 us
  Pallas kernels: 31.7 us -> 85 us
  waiting for transfers between devices: 51.1 us -> 23.4 us
  between operations: 14.9 us -> 1.44 us
  matrix products: 15 us -> 8.23 us
    psum x1 -> x0, blocking collectives: 65.2 us -> none  [on_device(): small = lax.psum(small, ('seq', 'batch'))]
    pallas_call x0 -> x1, Pallas kernels: none -> 53.9 us  [tail(): pl.pallas_call(functools.partial(tail_body, dims, norm), out_shape=(jax.S...]
    all_to_all x1 -> x0, blocking collectives: 30.8 us -> none  [on_device(): lax.all_to_all(features.reshape(rows, n, cols).transpose(1, 0, 2), 'seq',...]
    all_gather x1 -> x0, waiting for transfers between devices: 28 us -> none  [on_device(): every_delta = lax.all_gather(delta, 'seq', axis=0, tiled=True)]
    dot_general x3 -> x0, matrix products: 7.33 us -> none  [the longest x1 6.12 us: on_device(): lax.dot_general(f_mine, every_delta, (((0,), (0,)), ((), ())), preferred_...]
    all_to_all x1, waiting for transfers between devices: 16.7 us -> 23.4 us  [on_device(): lax.all_to_all(jnp.concatenate([q_send, k_send], axis=2), 'seq', 0, 0, ti...]
    all_to_all x1, waiting for transfers between devices: 6.3 us -> 0.01 us  [on_device(): lax.all_to_all(features.reshape(rows, chips, cols).transpose(1, 0, 2), 's...]
  transfers between devices with their start and end apart: 4 -> 2, of which waited for: 3 -> 1; matrix products, arithmetic and copies ran while one was open for 6% -> 9% of each run, Pallas kernels for 0% -> 21%
where the time goes in v2:
time: 149 us; the launch traced here: 147 us
  Pallas kernels  85 us (57%)
  waiting for transfers between devices  23.4 us (16%)
  starting transfers between devices  14.1 us (9%)
  local copies, waits for them, and re-layouts  9.75 us (7%)
  matrix products  8.23 us (6%)
  other arithmetic  5.02 us (3%)
    pallas_call x1, Pallas kernels, tail(): pl.pallas_call(functools.partial(tail_body, dims, norm), out_shape=(jax.S...  53.9 us
    pallas_call x1, Pallas kernels, attention(): pl.pallas_call(functools.partial(attn_body, tq, kc, sub, blocks, rows, sc...  31.1 us
    all_to_all x1, waiting for transfers between devices, on_device(): lax.all_to_all(jnp.concatenate([q_send, k_send], axis=2), 'seq', 0, 0, ti...  23.4 us
    all_to_all x1, starting transfers between devices, on_device(): lax.all_to_all(jnp.concatenate([q_send, k_send], axis=2), 'seq', 0, 0, ti...  9.72 us
    dot_general x1, matrix products, on_device(): pre = jnp.dot(features, w_in, preferred_element_type=jnp.float32) + b_in  7.45 us
    unnamed x19, local copies, waits for them, and re-layouts  4.86 us
    all_to_all x1, starting transfers between devices, on_device(): lax.all_to_all(features.reshape(rows, chips, cols).transpose(1, 0, 2), 's...  4.39 us
  transfers between devices with their start and end apart: 2, of which 1 were waited for; matrix products, arithmetic and copies ran while one was open for 9% of the time, Pallas kernels for 21%

profile of v2, /device:TPU:1, one launch (start us, length us, event | category | flops | bytes accessed | tf_op | source)
XLA Modules:
  0.0 146.9 jit_solution(14517267997395157835)
XLA Ops:
  0.6 1.0 copy.20
  1.7 1.6 %copy.15 = bf16[1,128,4096]{1,2,0:T(8,128)(2,1)S(1)} copy(bf16[1,128,4096]{2,1,0:T(8,128)(2,1)} %param.9) | data formatting | bytes 2097152 | tf_op args[0]
  3.3 0.7 copy.16
  4.0 0.2 broadcast_in_dim.2
  4.2 1.6 %pad_maximum_fusion = bf16[32,128,256]{2,1,0:T(8,128)(2,1)} fusion(bf16[32,128,128]{2,1,0:T(8,128)(2,1)S(1)} %bitcast.43, bf16[32,128,128]{2,1,0:T(8,128)(2,1)S(1)} %bitcast.44), kind=kLoop, calls=%fused_computation | loop fusion | flops 4194304 | bytes 4194304 | tf_op jit(solution)/shard_map/concatenate | solution.py:460
  5.8 0.0 copy-start.2
  5.8 0.0 copy-start.3
  5.8 9.7 %all-to-all-start = ((bf16[32,128,256]{2,1,0:T(8,128)(2,1)}), bf16[32,128,256]{2,1,0:T(8,128)(2,1)S(1)}, u32[]{:S(2)}, u32[]{:S(2)}) async-start(bf16[32,128,256]{2,1,0:T(8,128)(2,1)} %pad_maximum_fusion), calls=%async_computation | async-start | bytes 4194304 | tf_op jit(solution)/shard_map/all_to_all | solution.py:460
  16.2 0.0 copy-done.2
  16.2 0.0 copy-done.3
  16.2 1.1 pad_maximum_fusion.1
  17.3 0.0 copy-start
  17.3 1.4 copy.22
  18.7 0.0 copy-start.5
  18.7 0.0 copy-done
  18.7 0.6 fusion.3
  19.3 1.2 compare_convert_fusion.live_ref
  20.5 23.4 %all-to-all-done = bf16[32,128,256]{2,1,0:T(8,128)(2,1)S(1)} async-done(((bf16[32,128,256]{2,1,0:T(8,128)(2,1)}), bf16[32,128,256]{2,1,0:T(8,128)(2,1)S(1)}, u32[]{:S(2)}, u32[]{:S(2)}) %all-to-all-start) | async-done | bytes 2097184 | tf_op jit(solution)/shard_map/all_to_all | solution.py:460
  43.9 4.4 %all-to-all-start.1 = ((bf16[16,128,384]{2,1,0:T(8,128)(2,1)}), bf16[16,128,384]{2,1,0:T(8,128)(2,1)}, u32[]{:S(2)}, u32[]{:S(2)}) async-start(bf16[16,128,384]{2,1,0:T(8,128)(2,1)} %bitcast.38), calls=%async_computation.1 | async-start | bytes 3145728 | tf_op jit(solution)/shard_map/all_to_all | solution.py:466
  48.3 0.0 copy-done.5
  48.3 0.0 copy-start.4
  48.3 0.0 copy-start.6
  48.3 7.5 %add_multiply_fusion = (f32[128,1024]{1,0:T(8,128)}, bf16[128,1024]{1,0:T(8,128)(2,1)S(1)}) fusion(f32[1024]{0:T(1024)S(1)} %copy-done.5, bf16[6144,1024]{1,0:T(8,128)(2,1)} %param.14, bf16[128,1024]{1,0:T(8,128)(2,1)} %bitcast.50, bf16[128,1024]{1,0:T(8,128)(2,1)S(1)} %bitcast.47, bf16[128,4096]{1,0:T(8,128)(2,1)S(1)} %bitcast.41), kind=kOutput, calls=%fused_computation.6 | convolution fusion | flops 1616642048 | bytes 14946304 | tf_op jit(solution)/shard_map/dot_general | solution.py:469
  55.8 0.0 copy-start.7
  55.8 0.0 copy-done.4
  55.8 0.0 copy-done.6
  55.8 0.8 fusion.pred_ref
  56.5 0.6 fusion.2
  57.1 0.0 copy-done.7
  57.1 31.1 %mass.1.mass_ref = f32[32,1,128]{2,1,0:T(1,128)S(1)} custom-call(s32[32]{0:T(128)S(1)} %bitcast.37, s32[1]{0:T(128)} %copy.24.limit_ref, bf16[32,128,128]{2,1,0:T(8,128)(2,1)S(1)} %get-tuple-element.9.q_hbm, bf16[32,128,128]{2,1,0:T(8,128)(2,1)S(1)} %get-tuple-element.8.k_hbm), custom_call_target="tpu_custom_call" | custom-call | flops 2147483648 | bytes 2097152 | tf_op jit(solution)/shard_map/mass/pallas_call | solution.py:87
  88.3 0.0 copy-start.1
  88.3 0.6 copy-done.1
  88.9 0.0 all-to-all-done.1
  88.9 53.9 %tail.1 = (f32[48,1024]{1,0:T(8,128)}, f32[2,8,640]{2,1,0:T(8,128)}) custom-call(f32[32,1,128]{2,1,0:T(1,128)} %copy-done.1, f32[8,128]{1,0:T(8,128)} %fusion.pred_ref, f32[1,128]{1,0:T(1,128)} %compare_convert_fusion.live_ref, bf16[8,1024]{1,0:T(8,128)(2,1)} %bitcast.51, f32[128,1024]{1,0:T(8,128)} %get-tuple-element.10.slope_ref, ...), custom_call_target="tpu_custom_call" | custom-call | flops 1610612736 | bytes 8388608 | tf_op jit(solution)/shard_map/tail/pallas_call | solution.py:416
  142.7 0.8 slice_bitcast_fusion
  143.5 0.6 slice_bitcast_fusion.2
  144.1 0.6 slice_reduce_fusion
  144.7 0.6 fusion.1
  145.3 1.6 %copy.25 = f32[48,1024]{1,0:T(8,128)} copy(f32[48,1024]{1,0:T(8,128)} %get-tuple-element.18) | data formatting | bytes 393216
  (1 shorter events, 0.0 us)
Async XLA Ops:
  5.8 10.4 %copy-start.2 = (bf16[1,128,4096]{2,1,0:T(8,128)(2,1)S(1)}, bf16[1,128,4096]{2,1,0:T(8,128)(2,1)}, u32[]{:S(2)}) copy-start(bf16[1,128,4096]{2,1,0:T(8,128)(2,1)} %param.9) | copy-start | bytes 3145732
  5.8 10.4 %copy-start.3 = (bf16[1,128,1024]{2,1,0:T(8,128)(2,1)S(1)}, bf16[1,128,1024]{2,1,0:T(8,128)(2,1)}, u32[]{:S(2)}) copy-start(bf16[1,128,1024]{2,1,0:T(8,128)(2,1)} %param.10) | copy-start | bytes 786436
  5.8 38.1 %all-to-all-start = ((bf16[32,128,256]{2,1,0:T(8,128)(2,1)}), bf16[32,128,256]{2,1,0:T(8,128)(2,1)S(1)}, u32[]{:S(2)}, u32[]{:S(2)}) async-start(bf16[32,128,256]{2,1,0:T(8,128)(2,1)} %pad_maximum_fusion), calls=%async_computation | async-start | bytes 4194304 | tf_op jit(solution)/shard_map/all_to_all | solution.py:460
  17.3 1.4 copy-start
  18.7 29.6 %copy-start.5 = (f32[1024]{0:T(1024)S(1)}, f32[1024]{0:T(1024)}, u32[]{:S(2)}) copy-start(f32[1024]{0:T(1024)} %param.15) | copy-start | bytes 12292
  43.9 45.0 %all-to-all-start.1 = ((bf16[16,128,384]{2,1,0:T(8,128)(2,1)}), bf16[16,128,384]{2,1,0:T(8,128)(2,1)}, u32[]{:S(2)}, u32[]{:S(2)}) async-start(bf16[16,128,384]{2,1,0:T(8,128)(2,1)} %bitcast.38), calls=%async_computation.1 | async-start | bytes 3145728 | tf_op jit(solution)/shard_map/all_to_all | solution.py:466
  48.3 7.5 %copy-start.4 = (bf16[1024,8]{0,1:T(8,128)(2,1)S(1)}, bf16[1024,8]{0,1:T(8,128)(2,1)}, u32[]{:S(2)}) copy-start(bf16[1024,8]{0,1:T(8,128)(2,1)} %param.16) | copy-start | bytes 49156
  48.3 7.5 %copy-start.6 = (f32[8]{0:T(128)S(1)}, f32[8]{0:T(128)}, u32[]{:S(2)}) copy-start(f32[8]{0:T(128)} %param.17) | copy-start | bytes 100
  55.8 1.4 copy-start.7
  88.3 0.6 copy-start.1

commit v3 on v2

--- a/solution.py
+++ b/solution.py
@@ -87,7 +87,7 @@
     return pl.pallas_call(
         functools.partial(attn_body, tq, kc, sub, blocks, rows, scale2),
         out_shape=jax.ShapeDtypeStruct((blocks, 1, rows), jnp.float32),
-        in_specs=[pl.BlockSpec(memory_space=pltpu.SMEM)] * 2 + [pl.BlockSpec(memory_space=pl.ANY)] * 2,
+        in_specs=[pl.BlockSpec(memory_space=pltpu.SMEM)] * 2 + [pl.BlockSpec(memory_space=pltpu.HBM)] * 2,
         out_specs=pl.BlockSpec(memory_space=pltpu.VMEM),
         scratch_shapes=[
             pltpu.VMEM((total, head), jnp.bfloat16),
@@ -111,7 +111,165 @@
     )
 
 
-def tail_body(dims, norm, mass_ref, pred_ref, live_ref, w2t_ref, slope_ref, act_ref, f_ref, grad_ref, small_ref,
+def head_body(dims, per, q_ref, k_ref, v_ref, bin_ref, w2t_ref, bias_ref, w_hbm, qa, ka, pred_ref, slope_ref, act_ref,
+              stage, wbuf, pre, w_sem, i_send, i_recv, d_send, d_recv, l_sem):
+    ny, nz, nb = dims
+    chips = ny * nz
+    s, b = lax.axis_index("seq"), lax.axis_index("batch")
+    core, c = lax.rem(s, 2), s // 2
+    z, y = lax.rem(c, nz), c // nz
+    partner = (s + 1 - 2 * core, b)
+    head = ka.shape[2]
+    slots, deep, hidden = wbuf.shape
+    steps = w_hbm.shape[0] // deep
+
+    def w_copy(i):
+        at = lax.rem(i, slots)
+        return pltpu.make_async_copy(w_hbm.at[pl.ds(pl.multiple_of(i * deep, deep), deep), :], wbuf.at[at], w_sem.at[at])
+
+    for i in range(slots):
+        w_copy(i).start()
+
+    def chip_at(r, sign):
+        dy, dz = r // nz, lax.rem(r, nz)
+        return lax.rem(y + sign * dy + ny, ny) * nz + lax.rem(z + sign * dz + nz, nz)
+
+    barrier = pltpu.get_barrier_semaphore()
+
+    def greet(r, _):
+        pl.semaphore_signal(barrier, inc=1, device_id=(2 * chip_at(r, 1) + core, b), device_id_type=MESH)
+        return 0
+    lax.fori_loop(1, chips, greet, 0)
+    pl.semaphore_signal(barrier, inc=1, device_id=partner, device_id_type=MESH)
+    pl.semaphore_wait(barrier, chips)
+
+    def columns(ref, i):
+        return ref.at[:, pl.ds(pl.multiple_of(i * head, head), head)]
+
+    def parts(to):
+        return (columns(q_ref, 2 * to + core), columns(q_ref, 2 * to + 1 - core), columns(k_ref, (2 * to) // per))
+
+    def arrivals(frm):
+        return (qa.at[2 * frm + core], stage.at[0, frm], stage.at[1, frm])
+
+    def across(i, src, to, frm, dst):
+        return remote(src, dst, i_send.at[i, to], i_recv.at[i, frm], (2 * to + core, b))
+
+    def send(r, _):
+        to = chip_at(r, 1)
+        for i in (1, 2, 0):
+            across(i, parts(to)[i], to, c, arrivals(c)[i]).start()
+        return 0
+    lax.fori_loop(1, chips, send, 0)
+
+    def over(i, src, at):
+        dst = (qa.at[2 * at + core], ka.at[2 * at + core])[i]
+        return remote(src, dst, d_send.at[i, at], d_recv.at[i, at], partner)
+
+    def keep(src, at):
+        return pltpu.make_async_copy(src, ka.at[2 * at + core], l_sem.at[at])
+
+    own_q, other_q, own_k = parts(c)
+    over(0, other_q, c).start()
+    over(1, own_k, c).start()
+    keep(own_k, c).start()
+    own_copy = pltpu.make_async_copy(own_q, qa.at[2 * c + core], l_sem.at[chips])
+    own_copy.start()
+
+    pre[...] = jnp.broadcast_to(bin_ref[...], pre.shape)
+
+    def multiply(i, x):
+        w_copy(i).wait()
+        pre[...] += jnp.dot(x, wbuf[lax.rem(i, slots)], preferred_element_type=jnp.float32)
+
+    def refill(i):
+        @pl.when(i + slots < steps)
+        def _():
+            w_copy(i + slots).start()
+
+    base = 0
+    for ref in (q_ref, k_ref, v_ref):
+        def step(i, _, ref=ref, base=base):
+            multiply(base + i, ref[:, pl.ds(pl.multiple_of(i * deep, deep), deep)])
+            refill(base + i)
+            return 0
+        count = ref.shape[1] // deep
+        lax.fori_loop(0, count, step, 0)
+        base += count
+    p = pre[...]
+    sig = jax.nn.sigmoid(p)
+    act = (p * sig).astype(jnp.bfloat16)
+    act_ref[...] = act
+    slope_ref[...] = sig * (1.0 + p * (1.0 - sig))
+    out = lax.dot_general(w2t_ref[...], act, (((1,), (1,)), ((), ())), preferred_element_type=jnp.float32)
+    for g in range(pred_ref.shape[0]):
+        pred_ref[g:g + 1, :] = out[g:g + 1, :] + bias_ref[g]
+
+    def pass_on(r, _):
+        frm = chip_at(r, -1)
+        for i in (1, 2):
+            across(i, parts(frm)[i], frm, frm, arrivals(frm)[i]).wait_recv()
+            over(i - 1, stage.at[i - 1, frm], frm).start()
+        keep(stage.at[1, frm], frm).start()
+        return 0
+    lax.fori_loop(1, chips, pass_on, 0)
+
+    def settle(r, _):
+        frm = chip_at(r, -1)
+        to = chip_at(r, 1)
+        across(0, parts(frm)[0], frm, frm, arrivals(frm)[0]).wait_recv()
+        for i in range(3):
+            across(i, parts(to)[i], to, c, arrivals(c)[i]).wait_send()
+        return 0
+    lax.fori_loop(1, chips, settle, 0)
+
+    def settle_over(at, _):
+        for i in range(2):
+            dst = (qa.at[2 * at + 1 - core], ka.at[2 * at + 1 - core])[i]
+            remote(stage.at[i, at], dst, d_send.at[i, at], d_recv.at[i, at], partner).wait()
+        keep(stage.at[1, at], at).wait()
+        return 0
+    lax.fori_loop(0, chips, settle_over, 0)
+    own_copy.wait()
+
+
+def head(dims, q, k, v, b_in, w2t, bias, w_in, slots=3, deep=512):
+    ny, nz, nb = dims
+    rows, hidden = q.shape[0], w_in.shape[1]
+    heads = w2t.shape[0]
+    size = k.shape[1] // heads
+    chips = ny * nz
+    n = 2 * chips
+    vm, anywhere = pltpu.VMEM, pltpu.HBM
+    dma = pltpu.SemaphoreType.DMA
+    block = lambda space: pl.BlockSpec(memory_space=space)
+    return pl.pallas_call(
+        functools.partial(head_body, dims, q.shape[1] // k.shape[1]),
+        out_shape=(
+            jax.ShapeDtypeStruct((n, rows, size), jnp.bfloat16),
+            jax.ShapeDtypeStruct((n, rows, size), jnp.bfloat16),
+            jax.ShapeDtypeStruct((heads, rows), jnp.float32),
+            jax.ShapeDtypeStruct((rows, hidden), jnp.float32),
+            jax.ShapeDtypeStruct((rows, hidden), jnp.bfloat16),
+        ),
+        in_specs=[block(vm)] * 5 + [block(pltpu.SMEM), block(anywhere)],
+        out_specs=[block(anywhere)] * 2 + [block(vm)] * 3,
+        scratch_shapes=[
+            vm((2, chips, rows, size), jnp.bfloat16),
+            vm((slots, deep, hidden), jnp.bfloat16),
+            vm((rows, hidden), jnp.float32),
+            dma((slots,)),
+            dma((3, chips)), dma((3, chips)),
+            dma((2, chips)), dma((2, chips)),
+            dma((chips + 1,)),
+        ],
+        compiler_params=pltpu.CompilerParams(collective_id=1, has_side_effects=True, vmem_limit_bytes=56 * 2**20),
+        cost_estimate=pl.CostEstimate(flops=2 * rows * w_in.shape[0] * hidden, bytes_accessed=16 * 2**20, transcendentals=0),
+        name="head",
+    )(q, k, v, b_in, w2t, bias, w_in)
+
+
+def tail_body(dims, norm, order_ref, limit_ref, mass_ref, pred_ref, w2t_ref, slope_ref, act_ref, f_ref, grad_ref, small_ref,
               mrecv, lab, dl, ft, part, pair, xrecv, sm, smr, zs, ys, xs,
               m_send, m_recv, g_send, g_recv, p_send, p_recv, x_send, x_recv, s_send, s_recv):
     ny, nz, nb = dims
@@ -163,7 +321,9 @@
         for i in range(1, per):
             total = total + mrecv[per * g + i]
         lab[g:g + 1, :] = jnp.log1p(total)
-    resid_t = ((pred_ref[...] - lab[...]) * live_ref[...] * norm).astype(jnp.bfloat16)
+    position = order_ref[s] * rows + lax.broadcasted_iota(jnp.int32, (1, rows), 1)
+    live = jnp.where(position < limit_ref[0], 1.0, 0.0)
+    resid_t = ((pred_ref[...] - lab[...]) * live * norm).astype(jnp.bfloat16)
     resid = resid_t.astype(jnp.float32).T.astype(jnp.bfloat16)
     back = jnp.dot(resid, w2t_ref[...], preferred_element_type=jnp.float32)
     delta = (back * slope_ref[...]).astype(jnp.bfloat16)
@@ -402,7 +562,7 @@
     lax.fori_loop(1, n, mass_drain, 0)
 
 
-def tail(dims, norm, mass, pred_t, live, w2t, slope, act, f, chunks=2):
+def tail(dims, norm, order, limit, mass, pred_t, w2t, slope, act, f, chunks=2):
     ny, nz, nb = dims
     n = mass.shape[0]
     rows, hidden = slope.shape
@@ -419,7 +579,7 @@
             jax.ShapeDtypeStruct((half // nb, hidden), jnp.float32),
             jax.ShapeDtypeStruct((2, heads, sw), jnp.float32),
         ),
-        in_specs=[pl.BlockSpec(memory_space=vm)] * 7,
+        in_specs=[pl.BlockSpec(memory_space=pltpu.SMEM)] * 2 + [pl.BlockSpec(memory_space=vm)] * 6,
         out_specs=[pl.BlockSpec(memory_space=vm)] * 2,
         scratch_shapes=[
             vm((n, 1, rows), jnp.float32),
@@ -443,39 +603,31 @@
         compiler_params=pltpu.CompilerParams(collective_id=3, has_side_effects=True, vmem_limit_bytes=56 * 2**20),
         cost_estimate=pl.CostEstimate(flops=2 * tokens * feats * hidden, bytes_accessed=8 * 2**20, transcendentals=0),
         name="tail",
-    )(mass, pred_t, live, w2t, slope, act, f)
+    )(order, limit, mass, pred_t, w2t, slope, act, f)
 
 
 def on_device(dims, queries, keys, values, lengths, block_pos, w_in, b_in, output_weight, output_bias):
     q_rows, k_rows, v_rows = queries[0], keys[0], values[0]
     rows = q_rows.shape[0]
     hidden, heads_kv = output_weight.shape
-    head = k_rows.shape[1] // heads_kv
     n = lax.axis_size("seq")
-    per = q_rows.shape[1] // k_rows.shape[1]
     total = n * rows
-    mine = lax.axis_index("seq")
-    q_send = q_rows.reshape(rows, n, head).transpose(1, 0, 2)
-    k_send = jnp.repeat(k_rows.reshape(rows, heads_kv, head).transpose(1, 0, 2), per, axis=0)
-    both = lax.all_to_all(jnp.concatenate([q_send, k_send], axis=2), "seq", 0, 0, tiled=True)
-    mass_own = attention(block_pos[0], lengths, both[:, :, :head], both[:, :, head:], 512, 512, 64)
+    w2t = output_weight.T
+    q_all, k_all, pred_t, slope, act = head(
+        dims, q_rows, k_rows, v_rows, b_in[None, :], w2t, output_bias, w_in
+    )
     features = jnp.concatenate([q_rows, k_rows, v_rows], axis=1)
     chips = n // 2
     cols = features.shape[1] // chips
+    f_send = features.reshape(rows, chips, cols).transpose(1, 0, 2)
+    f_send, pred_t = lax.optimization_barrier((f_send, pred_t))
     planes = [[2 * i + core for i in range(chips)] for core in range(2)]
     f_mine = lax.all_to_all(
-        features.reshape(rows, chips, cols).transpose(1, 0, 2), "seq", 0, 0, tiled=True, axis_index_groups=planes
+        f_send, "seq", 0, 0, tiled=True, axis_index_groups=planes
     ).reshape(chips * rows, cols)
-    pre = jnp.dot(features, w_in, preferred_element_type=jnp.float32) + b_in
-    sig = jax.nn.sigmoid(pre)
-    act = (pre * sig).astype(jnp.bfloat16)
-    slope = sig * (1.0 + pre * (1.0 - sig))
-    pred = jnp.dot(act, output_weight, preferred_element_type=jnp.float32) + output_bias
-    offsets = jnp.arange(rows, dtype=jnp.int32)
-    query_pos = lax.dynamic_index_in_dim(block_pos[0], mine, 0, keepdims=False) * rows + offsets
-    query_live = (query_pos < lengths[0]).astype(jnp.float32)
+    mass_own = attention(block_pos[0], lengths, q_all, k_all, 512, 512, 64)
     norm = 1.0 / math.sqrt(lax.axis_size("batch") * total)
-    grad_w_in, small = tail(dims, norm, mass_own, pred.T, query_live[None, :], output_weight.T, slope, act, f_mine)
+    grad_w_in, small = tail(dims, norm, block_pos[0], lengths, mass_own, pred_t, w2t, slope, act, f_mine)
     small = jnp.concatenate([small[0], small[1]], axis=1)
     grad_b_in = small[:, hidden:hidden + 128].reshape(hidden)
     return (grad_w_in, grad_b_in, small[:, :hidden].T, small[:, hidden + 128])

time: 149 us -> 136 us (0.913)
  Pallas kernels: 85 us -> 119 us
  waiting for transfers between devices: 23.4 us -> 0.01 us
  matrix products: 8.23 us -> 0 us
  starting transfers between devices: 14.1 us -> 6.07 us
  local copies, waits for them, and re-layouts: 9.75 us -> 5.61 us
  other arithmetic: 5.02 us -> 2.11 us
    pallas_call x0 -> x1, Pallas kernels: none -> 35.4 us  [head(): pl.pallas_call(functools.partial(head_body, dims, q.shape[1] // k.shape[1...]
    all_to_all x2 -> x1, waiting for transfers between devices: 23.4 us -> 0.01 us  [on_device(): lax.all_to_all(f_send, 'seq', 0, 0, tiled=True, axis_index_groups=planes)]
    dot_general x2 -> x0, matrix products: 8.23 us -> none  [the longest x1 7.45 us: on_device(): pre = jnp.dot(features, w_in, preferred_element_type=jnp.float32) + b_in]
    all_to_all x2 -> x1, starting transfers between devices: 14.1 us -> 6.07 us  [on_device(): lax.all_to_all(f_send, 'seq', 0, 0, tiled=True, axis_index_groups=planes)]
    unnamed x19 -> x9, local copies, waits for them, and re-layouts: 4.86 us -> 2.23 us
    concatenate x1 -> x0, other arithmetic: 1.58 us -> none  [on_device(): jnp.concatenate([q_send, k_send], axis=2)]
  transfers between devices with their start and end apart: 2 -> 1, of which waited for: 1 -> 0; matrix products, arithmetic and copies ran while one was open for 9% -> 0% of each run, Pallas kernels for 21% -> 23%
where the time goes in v3:
time: 136 us; the launch traced here: 134 us
  Pallas kernels  119 us (88%)
  starting transfers between devices  6.07 us (4%)
  local copies, waits for them, and re-layouts  5.61 us (4%)
  other arithmetic  2.11 us (2%)
  between operations  1.37 us (1%)
    pallas_call x1, Pallas kernels, tail(): pl.pallas_call(functools.partial(tail_body, dims, norm), out_shape=(jax.S...  52.7 us
    pallas_call x1, Pallas kernels, head(): pl.pallas_call(functools.partial(head_body, dims, q.shape[1] // k.shape[1...  35.4 us
    pallas_call x1, Pallas kernels, attention(): pl.pallas_call(functools.partial(attn_body, tq, kc, sub, blocks, rows, sc...  31.1 us
    all_to_all x1, starting transfers between devices, on_device(): lax.all_to_all(f_send, 'seq', 0, 0, tiled=True, axis_index_groups=planes)  6.07 us
  transfers between devices with their start and end apart: 1, of which 0 were waited for; matrix products, arithmetic and copies ran while one was open for 0% of the time, Pallas kernels for 23%

profile of v3, /device:TPU:1, one launch (start us, length us, event | category | flops | bytes accessed | tf_op | source)
XLA Modules:
  0.0 134.4 jit_solution(6333395721653434126)
XLA Ops:
  0.6 1.5 %pad_maximum_fusion = bf16[128,6144]{1,0:T(8,128)(2,1)S(1)} fusion(bf16[128,1024]{1,0:T(8,128)(2,1)} %bitcast.30, bf16[128,1024]{1,0:T(8,128)(2,1)} %bitcast.28, bf16[128,4096]{1,0:T(8,128)(2,1)} %bitcast.26), kind=kLoop, calls=%fused_computation.1 | loop fusion | flops 4718592 | bytes 3145728 | tf_op jit(solution)/shard_map/concatenate | solution.py:619
  2.1 1.4 %copy.17 = bf16[16,16,8,384]{3,2,0,1:T(8,128)(2,1)} copy(bf16[16,16,8,384]{3,2,1,0:T(8,128)(2,1)S(1)} %bitcast.25) | data formatting | bytes 3145728 | tf_op jit(solution)/shard_map/reshape | solution.py:622
  3.5 35.4 %head.1 = (bf16[32,128,128]{2,1,0:T(8,128)(2,1)}, bf16[32,128,128]{2,1,0:T(8,128)(2,1)}, f32[8,128]{1,0:T(8,128)}, f32[128,1024]{1,0:T(8,128)}, bf16[128,1024]{1,0:T(8,128)(2,1)}) custom-call(bf16[128,4096]{1,0:T(8,128)(2,1)} %bitcast.27, bf16[128,1024]{1,0:T(8,128)(2,1)} %bitcast.29, bf16[128,1024]{1,0:T(8,128)(2,1)} %bitcast.31, f32[1,1024]{1,0:T(1,128)} %bitcast.34, ...), custom_call_target="tpu_custom_call" | custom-call | flops 1610612736 | bytes 16777216 | tf_op jit(solution)/shard_map/head/pallas_call | solution.py:246
  39.0 0.0 copy-start
  39.0 0.0 copy-start.1
  39.0 0.0 copy-start.2
  39.0 6.1 %all-to-all-start = ((bf16[16,128,384]{2,1,0:T(8,128)(2,1)}), bf16[16,128,384]{2,1,0:T(8,128)(2,1)}, u32[]{:S(2)}, u32[]{:S(2)}) async-start(bf16[16,128,384]{2,1,0:T(8,128)(2,1)} %bitcast.24), calls=%async_computation | async-start | bytes 3145728 | tf_op jit(solution)/shard_map/all_to_all | solution.py:625
  45.7 0.0 copy-done
  45.7 0.0 copy-done.1
  45.7 0.0 copy-done.2
  45.8 31.1 %mass.1.mass_ref = f32[32,1,128]{2,1,0:T(1,128)S(1)} custom-call(s32[32]{0:T(128)S(1)} %bitcast.23, s32[1]{0:T(128)S(6)} %copy.19.limit_ref, bf16[32,128,128]{2,1,0:T(8,128)(2,1)S(1)} %copy-done, bf16[32,128,128]{2,1,0:T(8,128)(2,1)S(1)} %copy-done.1), custom_call_target="tpu_custom_call" | custom-call | flops 2147483648 | bytes 2097152 | tf_op jit(solution)/shard_map/mass/pallas_call | solution.py:87
  76.9 0.0 copy-start.3
  76.9 0.6 copy-done.3
  77.5 0.0 all-to-all-done
  77.5 52.7 %tail.1 = (f32[48,1024]{1,0:T(8,128)}, f32[2,8,640]{2,1,0:T(8,128)}) custom-call(s32[32]{0:T(128)} %bitcast.22, s32[1]{0:T(128)S(6)} %copy.19.limit_ref, f32[32,1,128]{2,1,0:T(1,128)} %copy-done.3, f32[8,128]{1,0:T(8,128)} %get-tuple-element.16.pred_ref, bf16[8,1024]{1,0:T(8,128)(2,1)} %bitcast.33, f32[128,1024]{1,0:T(8,128)} %get-tuple-element.17.slope_ref, ...), custom_call_target="tpu_custom_call" | custom-call | flops 1610612736 | bytes 8388608 | tf_op jit(solution)/shard_map/tail/pallas_call | solution.py:576
  130.2 0.8 slice_bitcast_fusion
  130.9 0.6 slice_bitcast_fusion.2
  131.5 0.6 slice_reduce_fusion
  132.2 0.6 fusion
  132.8 1.6 %copy.20 = f32[48,1024]{1,0:T(8,128)} copy(f32[48,1024]{1,0:T(8,128)} %get-tuple-element.28) | data formatting | bytes 393216
Async XLA Ops:
  39.0 6.8 %copy-start = (bf16[32,128,128]{2,1,0:T(8,128)(2,1)S(1)}, bf16[32,128,128]{2,1,0:T(8,128)(2,1)}, u32[]{:S(2)}) copy-start(bf16[32,128,128]{2,1,0:T(8,128)(2,1)} %get-tuple-element.13.q_hbm) | copy-start | bytes 3145732
  39.0 6.8 %copy-start.1 = (bf16[32,128,128]{2,1,0:T(8,128)(2,1)S(1)}, bf16[32,128,128]{2,1,0:T(8,128)(2,1)}, u32[]{:S(2)}) copy-start(bf16[32,128,128]{2,1,0:T(8,128)(2,1)} %get-tuple-element.14.k_hbm) | copy-start | bytes 3145732
  39.0 6.8 %copy-start.2 = (s32[1,32]{1,0:T(1,128)S(1)}, s32[1,32]{1,0:T(1,128)}, u32[]{:S(2)}) copy-start(s32[1,32]{1,0:T(1,128)} %param.13) | copy-start | bytes 388
  39.0 38.5 %all-to-all-start = ((bf16[16,128,384]{2,1,0:T(8,128)(2,1)}), bf16[16,128,384]{2,1,0:T(8,128)(2,1)}, u32[]{:S(2)}, u32[]{:S(2)}) async-start(bf16[16,128,384]{2,1,0:T(8,128)(2,1)} %bitcast.24), calls=%async_computation | async-start | bytes 3145728 | tf_op jit(solution)/shard_map/all_to_all | solution.py:625
  76.9 0.6 copy-start.3

commit v4 on v3

--- a/solution.py
+++ b/solution.py
@@ -4,10 +4,92 @@
 from jax.experimental import pallas as pl
 from jax.experimental.pallas import tpu as pltpu
 from jax.sharding import PartitionSpec as P
-
 NEG = -1e30
 
-def attn_body(tq, kc, sub, blocks, rows, scale2, order_ref, limit_ref, q_hbm, k_hbm, out_ref, qs, ks, s_ref, acc_ref, sems):
+def attn_core(tq, sub, total, scale2, limit, qs, ks, s_ref, acc_ref):
+    lanes = 128
+    groups = tq // lanes
+    nt = total // tq
+    eights = lambda x: x.reshape(x.shape[0] // 8, 8, tq)
+
+    def at(j, n=tq):
+        return pl.ds(pl.multiple_of(j * n, n), n)
+
+    def scores(i, j, mx, masked):
+        s = lax.dot_general(ks[at(j), :], qs[at(i), :], (((1,), (1,)), ((), ())), preferred_element_type=jnp.float32)
+        if masked:
+            kp = lax.broadcasted_iota(jnp.int32, (tq, tq), 0)
+            qp = lax.broadcasted_iota(jnp.int32, (tq, tq), 1)
+            s = jnp.where(kp <= qp, s, NEG)
+        s_ref[lax.rem(i, 3), at(j), :] = s
+        return jnp.maximum(mx, jnp.max(eights(s), axis=0))
+
+    def weights(i, j, l, top):
+        for u in range(tq // sub):
+            here = pl.ds(pl.multiple_of(j * tq + u * sub, sub), sub)
+            w = jnp.exp2((eights(s_ref[lax.rem(i, 3), here, :]) - top[None]) * scale2)
+            s_ref[lax.rem(i, 3), here, :] = w.reshape(sub, tq)
+            l = l + jnp.sum(w, axis=0)
+        return l
+
+    def shares(i, j, rec):
+        for u in range(tq // sub):
+            here = pl.ds(pl.multiple_of(j * tq + u * sub, sub), sub)
+            w = (eights(s_ref[lax.rem(i, 3), here, :]) * rec[None]).reshape(sub, tq)
+            tot = w[:, :lanes]
+            for g in range(1, groups):
+                tot = tot + w[:, g * lanes:(g + 1) * lanes]
+            acc_ref[here, :] += tot
+
+    none = jnp.full((8, tq), NEG, jnp.float32)
+    zero = jnp.zeros((8, tq), jnp.float32)
+
+    def spread_top(mx):
+        return jnp.broadcast_to(jnp.max(mx, axis=0, keepdims=True), (8, tq))
+
+    def spread_rec(i, l):
+        pos = i * tq + lax.broadcasted_iota(jnp.int32, (1, tq), 1)
+        rec = jnp.where(pos < limit, 1.0 / jnp.sum(l, axis=0, keepdims=True), 0.0)
+        return jnp.broadcast_to(rec, (8, tq))
+
+    def step(i, top, rec, with_scores=True, with_weights=True, with_shares=True):
+        def each(j, carry):
+            mx, l = carry
+            if with_scores:
+                mx = scores(i, j, mx, False)
+            if with_weights:
+                l = weights(i + 1, j, l, top)
+            if with_shares:
+                shares(i + 2, j, rec)
+            return mx, l
+        mx, l = lax.fori_loop(0, i, each, (none, zero))
+        if with_scores:
+            mx = scores(i, i, mx, True)
+        if with_weights:
+            for d in (0, 1):
+                if with_scores or d:
+                    l = weights(i + 1, i + d, l, top)
+        if with_shares:
+            for d in (0, 1, 2):
+                if with_scores or with_weights and d or d == 2:
+                    shares(i + 2, i + d, rec)
+        return mx, l
+
+    last = nt - 1
+    mx, _ = step(last, none, none, True, False, False)
+    mx, l = step(last - 1, spread_top(mx), none, True, True, False)
+
+    def generic(t, carry):
+        top, rec = carry
+        i = last - t
+        mx, l = step(i, top, rec)
+        return spread_top(mx), spread_rec(i + 1, l)
+    top, rec = lax.fori_loop(2, nt, generic, (spread_top(mx), spread_rec(last, l)))
+    _, l = step(-1, top, rec, False, True, True)
+    step(-2, none, spread_rec(0, l), False, False, True)
+
+
+def attn_body(tq, sub, blocks, rows, scale2, order_ref, limit_ref, q_hbm, k_hbm, out_ref, qs, ks, s_ref, acc_ref, sems):
     total = blocks * rows
     def issue(s, _):
         p = order_ref[s]
@@ -19,58 +101,7 @@
     acc_ref[...] = jnp.zeros_like(acc_ref)
     for src, dst, i in ((q_hbm, qs, 0), (k_hbm, ks, 1)):
         pltpu.make_async_copy(src, src, sems.at[i]).wait()
-    limit = limit_ref[0]
-    lanes = 128
-    groups = tq // lanes
-
-    def tile(i, _):
-        q0 = pl.multiple_of(i * tq, tq)
-        q_part = qs[pl.ds(q0, tq), :]
-
-        def scores(r0, mx, masked):
-            k_part = ks[pl.ds(r0, kc), :]
-            s = lax.dot_general(k_part, q_part, (((1,), (1,)), ((), ())), preferred_element_type=jnp.float32)
-            if masked:
-                kp = r0 + lax.broadcasted_iota(jnp.int32, (kc, tq), 0)
-                qp = q0 + lax.broadcasted_iota(jnp.int32, (kc, tq), 1)
-                s = jnp.where(kp <= qp, s, NEG)
-            s_ref[pl.ds(r0, kc), :] = s
-            return jnp.maximum(mx, jnp.max(s.reshape(kc // 8, 8, tq), axis=0))
-
-        n_full = i * (tq // kc)
-        mx = lax.fori_loop(0, n_full, lambda j, m: scores(pl.multiple_of(j * kc, kc), m, False), jnp.full((8, tq), NEG, jnp.float32))
-        for d in range(tq // kc):
-            mx = scores(pl.multiple_of(q0 + d * kc, kc), mx, True)
-        top = jnp.max(mx, axis=0, keepdims=True)
-        top8 = jnp.broadcast_to(top, (8, tq))
-        n_sub = (i + 1) * (tq // sub)
-
-        def weights(j, l):
-            r0 = pl.multiple_of(j * sub, sub)
-            s = s_ref[pl.ds(r0, sub), :].reshape(sub // 8, 8, tq)
-            w = jnp.exp2((s - top8[None]) * scale2)
-            s_ref[pl.ds(r0, sub), :] = w.reshape(sub, tq)
-            return l + jnp.sum(w, axis=0)
-
-        l = lax.fori_loop(0, n_sub, weights, jnp.zeros((8, tq), jnp.float32))
-        denom = jnp.sum(l, axis=0, keepdims=True)
-        qpos = q0 + lax.broadcasted_iota(jnp.int32, (1, tq), 1)
-        rec = jnp.where(qpos < limit, 1.0 / denom, 0.0)
-        rec8 = jnp.broadcast_to(rec, (8, tq))
-
-        def shares(j, _):
-            r0 = pl.multiple_of(j * sub, sub)
-            w = s_ref[pl.ds(r0, sub), :].reshape(sub // 8, 8, tq) * rec8[None]
-            w = w.reshape(sub, tq)
-            tot = w[:, :lanes]
-            for g in range(1, groups):
-                tot = tot + w[:, g * lanes:(g + 1) * lanes]
-            acc_ref[pl.ds(r0, sub), :] += tot
-            return 0
-        lax.fori_loop(0, n_sub, shares, 0)
-        return 0
-
-    lax.fori_loop(0, total // tq, tile, 0)
+    attn_core(tq, sub, total, scale2, limit_ref[0], qs, ks, s_ref, acc_ref)
 
     def emit(s, _):
         p = order_ref[s]
@@ -80,23 +111,23 @@
     lax.fori_loop(0, blocks, emit, 0)
 
 
-def attention(order, limit, q_all, k_all, tq=512, kc=128, sub=64):
+def attention(order, limit, q_all, k_all, tq=512, sub=64):
     blocks, rows, head = q_all.shape
     total = blocks * rows
     scale2 = math.log2(math.e) / math.sqrt(head)
     return pl.pallas_call(
-        functools.partial(attn_body, tq, kc, sub, blocks, rows, scale2),
+        functools.partial(attn_body, tq, sub, blocks, rows, scale2),
         out_shape=jax.ShapeDtypeStruct((blocks, 1, rows), jnp.float32),
         in_specs=[pl.BlockSpec(memory_space=pltpu.SMEM)] * 2 + [pl.BlockSpec(memory_space=pltpu.HBM)] * 2,
         out_specs=pl.BlockSpec(memory_space=pltpu.VMEM),
         scratch_shapes=[
             pltpu.VMEM((total, head), jnp.bfloat16),
             pltpu.VMEM((total, head), jnp.bfloat16),
-            pltpu.VMEM((total, tq), jnp.float32),
+            pltpu.VMEM((3, total, tq), jnp.float32),
             pltpu.VMEM((total, 128), jnp.float32),
             pltpu.SemaphoreType.DMA((2,)),
         ],
-        compiler_params=pltpu.CompilerParams(vmem_limit_bytes=48 * 2**20),
+        compiler_params=pltpu.CompilerParams(vmem_limit_bytes=56 * 2**20),
         cost_estimate=pl.CostEstimate(flops=total * total * head, bytes_accessed=4 * total * head, transcendentals=total * total // 2),
         name="mass",
     )(order, limit, q_all, k_all)
@@ -269,8 +300,8 @@
     )(q, k, v, b_in, w2t, bias, w_in)
 
 
-def tail_body(dims, norm, order_ref, limit_ref, mass_ref, pred_ref, w2t_ref, slope_ref, act_ref, f_ref, grad_ref, small_ref,
-              mrecv, lab, dl, ft, part, pair, xrecv, sm, smr, zs, ys, xs,
+def tail_body(dims, norm, order_ref, limit_ref, mass_ref, pred_ref, w2t_ref, slope_ref, act_ref, f_ref, grad_ref, ow_ref, b_ref, bias_ref,
+              mrecv, lab, dl, ft, part, pair, xrecv, sm, small, smr, zs, ys, xs,
               m_send, m_recv, g_send, g_recv, p_send, p_recv, x_send, x_recv, s_send, s_recv):
     ny, nz, nb = dims
     n = ny * nz * 2
@@ -278,8 +309,9 @@
     core, c = lax.rem(s, 2), s // 2
     z, y = lax.rem(c, nz), c // nz
     rows, hidden = slope_ref.shape
-    chunks, tokens, width = dl.shape
-    feats = part.shape[1]
+    chunks, tokens = len(dl), dl[0].shape[0]
+    feats = part[0].shape[0]
+    begin = [sum(d.shape[1] for d in dl[:j]) for j in range(chunks + 1)]
     half = feats // 2
     own_rows = half // nb
     partner = (s + 1 - 2 * core, b)
@@ -329,7 +361,7 @@
     delta = (back * slope_ref[...]).astype(jnp.bfloat16)
     here = pl.ds(pl.multiple_of(c * rows, rows), rows)
     for j in range(chunks):
-        dl[j, here, :] = delta[:, j * width:(j + 1) * width]
+        dl[j][here, :] = delta[:, begin[j]:begin[j + 1]]
 
     wide = rows // 2
     slot = {}
@@ -349,7 +381,7 @@
     def piece(j, block, half_id, quarter):
         r0 = half_id * wide + (quarter * (wide // 2) if quarter is not None else 0)
         size = wide // 2 if quarter is not None else wide
-        return dl.at[j, pl.ds(pl.multiple_of(block * rows + r0, wide // 2), size), :]
+        return dl[j].at[pl.ds(pl.multiple_of(block * rows + r0, wide // 2), size), :]
 
     def neighbour(half_id, which, d):
         along_y = (half_id == 0) == (which == 0)
@@ -432,11 +464,11 @@
                 second_end(j, h, da)
 
     def multiply(j):
-        part[j] = jnp.dot(ft[...], dl[j], preferred_element_type=jnp.float32)
+        part[j][...] = jnp.dot(ft[...], dl[j][...], preferred_element_type=jnp.float32)
 
     def pair_copy(j, of):
-        ref = part.at[j, pl.ds(pl.multiple_of((1 - of) * half, half), half), :]
-        return remote(ref, pair.at[j], p_send.at[j], p_recv.at[j], partner)
+        ref = part[j].at[pl.ds(pl.multiple_of((1 - of) * half, half), half), :]
+        return remote(ref, pair[j], p_send.at[j], p_recv.at[j], partner)
 
     def pair_start(j):
         one = pair_copy(j, core)
@@ -445,12 +477,12 @@
 
     def x_copy(j, r):
         to = lax.rem(b + r, nb)
-        ref = pair.at[j, pl.ds(pl.multiple_of(to * own_rows, own_rows), own_rows), :]
-        return remote(ref, xrecv.at[j, r - 1], x_send.at[j, r - 1], x_recv.at[j, r - 1], (s, to))
+        ref = pair[j].at[pl.ds(pl.multiple_of(to * own_rows, own_rows), own_rows), :]
+        return remote(ref, xrecv[j].at[r - 1], x_send.at[j, r - 1], x_recv.at[j, r - 1], (s, to))
 
     def x_start(j):
         pair_copy(j, core).wait_recv()
-        pair[j] = pair[j] + part[j, pl.ds(pl.multiple_of(core * half, half), half), :]
+        pair[j][...] = pair[j][...] + part[j][pl.ds(pl.multiple_of(core * half, half), half), :]
         for r in (2, 1, 3)[: nb - 1]:
             one = x_copy(j, r)
             one.start()
@@ -459,23 +491,25 @@
     def x_end(j):
         for r in range(1, nb):
             x_copy(j, r).wait_recv()
-        own = pair[j, pl.ds(pl.multiple_of(b * own_rows, own_rows), own_rows), :]
+        own = pair[j][pl.ds(pl.multiple_of(b * own_rows, own_rows), own_rows), :]
         for r in range(1, nb):
-            own = own + xrecv[j, r - 1]
-        grad_ref[:, j * width:(j + 1) * width] = own
+            own = own + xrecv[j][r - 1]
+        grad_ref[:, begin[j]:begin[j + 1]] = own
 
     def small_start0():
         sw = sm.shape[2]
         out_term = jnp.dot(resid_t, act_ref[...], preferred_element_type=jnp.float32)
         sums = jnp.sum(delta.astype(jnp.float32), axis=0, keepdims=True)
-        bias = jnp.sum(resid_t.astype(jnp.float32), axis=1, keepdims=True)
+        bias = jnp.sum(resid.astype(jnp.float32), axis=0, keepdims=True)
         lanes = 128
         cols = [out_term[:, k * lanes:(k + 1) * lanes] for k in range(hidden // lanes)]
         cols.append(jnp.concatenate([sums[:, k * lanes:(k + 1) * lanes] for k in range(hidden // lanes)], axis=0))
-        cols.append(jnp.broadcast_to(bias, (heads, lanes)))
+        cols.append(jnp.zeros((heads, lanes), jnp.float32))
         each = sw // lanes
         for k, value in enumerate(cols):
             sm[k // each, :, (k % each) * lanes:(k % each + 1) * lanes] = value
+        at = (len(cols) - 1) % each * lanes
+        sm[1, 0:1, at:at + heads] = bias
         one = remote(sm.at[1 - core], smr, s_send.at[0], s_recv.at[0], partner)
         one.start()
         started.append(one)
@@ -512,46 +546,24 @@
 
     def small4():
         sm[core] = small_sum(2, xs, b, nb, to_x)
-        one = remote(sm.at[core], small_ref.at[core], s_send.at[10], s_recv.at[10], partner)
+        one = remote(sm.at[core], small.at[core], s_send.at[10], s_recv.at[10], partner)
         one.start()
         started.append(one)
-        small_ref[core] = sm[core]
+        small[core] = sm[core]
 
     def small5():
-        remote(sm.at[1 - core], small_ref.at[1 - core], s_send.at[10], s_recv.at[10], partner).wait_recv()
-
-    if chunks == 2:
-        stage0(0); small_start0(); stage1(0); stage2(0); stage0(1); stage3(0); small1(); stage1(1); stage4(0)
-        stage2(1); stage5(0); small2(); stage3(1)
-        multiply(0); pair_start(0); stage4(1); small3()
-        x_start(0); stage5(1)
-        multiply(1); pair_start(1); small4(); x_end(0); x_start(1); small5(); x_end(1)
-    else:
-        small = [small1, small2, small3, small4, small5]
-        stage0(0); small_start0(); stage1(0); stage2(0)
-        for j in range(chunks):
-            last = j + 1 == chunks
-            if not last:
-                stage0(j + 1)
-            stage3(j)
-            if not last:
-                stage1(j + 1)
-            stage4(j)
-            if not last:
-                stage2(j + 1)
-            stage5(j)
-            if small:
-                small.pop(0)()
-            multiply(j)
-            pair_start(j)
-            if small:
-                small.pop(0)()
-            if j > 0:
-                x_end(j - 1)
-            x_start(j)
-        for one in small:
-            one()
-        x_end(chunks - 1)
+        remote(sm.at[1 - core], small.at[1 - core], s_send.at[10], s_recv.at[10], partner).wait_recv()
+        sw = small.shape[2]
+        ow_ref[:, :sw] = small[0]
+        ow_ref[:, sw:] = small[1, :, :hidden - sw]
+        b_ref[...] = small[1, :, hidden - sw:hidden - sw + 128]
+        bias_ref[...] = small[1, 0:1, hidden - sw + 128:hidden - sw + 128 + heads]
+
+    stage0(0); small_start0(); stage1(0); stage2(0); stage0(1); stage3(0); small1(); stage1(1); stage4(0)
+    stage2(1); stage5(0); small2(); stage3(1)
+    multiply(0); pair_start(0); stage4(1); small3()
+    x_start(0); stage5(1)
+    multiply(1); pair_start(1); small4(); x_end(0); x_start(1); small5(); x_end(1)
 
     for one in started:
         one.wait_send()
@@ -562,13 +574,13 @@
     lax.fori_loop(1, n, mass_drain, 0)
 
 
-def tail(dims, norm, order, limit, mass, pred_t, w2t, slope, act, f, chunks=2):
+def tail(dims, norm, order, limit, mass, pred_t, w2t, slope, act, f, widths=(640, 384)):
     ny, nz, nb = dims
     n = mass.shape[0]
     rows, hidden = slope.shape
     tokens, feats = f.shape
     heads = pred_t.shape[0]
-    width = hidden // chunks
+    chunks = len(widths)
     half = feats // 2
     sw = (hidden + 256) // 2
     vm = pltpu.VMEM
@@ -577,18 +589,21 @@
         functools.partial(tail_body, dims, norm),
         out_shape=(
             jax.ShapeDtypeStruct((half // nb, hidden), jnp.float32),
-            jax.ShapeDtypeStruct((2, heads, sw), jnp.float32),
+            jax.ShapeDtypeStruct((heads, hidden), jnp.float32),
+            jax.ShapeDtypeStruct((heads, 128), jnp.float32),
+            jax.ShapeDtypeStruct((1, heads), jnp.float32),
         ),
         in_specs=[pl.BlockSpec(memory_space=pltpu.SMEM)] * 2 + [pl.BlockSpec(memory_space=vm)] * 6,
-        out_specs=[pl.BlockSpec(memory_space=vm)] * 2,
+        out_specs=[pl.BlockSpec(memory_space=vm)] * 4,
         scratch_shapes=[
             vm((n, 1, rows), jnp.float32),
             vm((heads, rows), jnp.float32),
-            vm((chunks, tokens, width), jnp.bfloat16),
+            tuple(vm((tokens, w), jnp.bfloat16) for w in widths),
             vm((feats, tokens), jnp.bfloat16),
-            vm((chunks, feats, width), jnp.float32),
-            vm((chunks, half, width), jnp.float32),
-            vm((chunks, nb - 1, half // nb, width), jnp.float32),
+            tuple(vm((feats, w), jnp.float32) for w in widths),
+            tuple(vm((half, w), jnp.float32) for w in widths),
+            tuple(vm((nb - 1, half // nb, w), jnp.float32) for w in widths),
+            vm((2, heads, sw), jnp.float32),
             vm((2, heads, sw), jnp.float32),
             vm((heads, sw), jnp.float32),
             vm((nz, heads, sw), jnp.float32),
@@ -625,12 +640,10 @@
     f_mine = lax.all_to_all(
         f_send, "seq", 0, 0, tiled=True, axis_index_groups=planes
     ).reshape(chips * rows, cols)
-    mass_own = attention(block_pos[0], lengths, q_all, k_all, 512, 512, 64)
+    mass_own = attention(block_pos[0], lengths, q_all, k_all, 512, 128)
     norm = 1.0 / math.sqrt(lax.axis_size("batch") * total)
-    grad_w_in, small = tail(dims, norm, block_pos[0], lengths, mass_own, pred_t, w2t, slope, act, f_mine)
-    small = jnp.concatenate([small[0], small[1]], axis=1)
-    grad_b_in = small[:, hidden:hidden + 128].reshape(hidden)
-    return (grad_w_in, grad_b_in, small[:, :hidden].T, small[:, hidden + 128])
+    grad_w_in, ow, gb, bias = tail(dims, norm, block_pos[0], lengths, mass_own, pred_t, w2t, slope, act, f_mine)
+    return (grad_w_in, gb.reshape(hidden), ow.T, bias.reshape(heads_kv))
 
 
 def solution(mesh):

time: 136 us -> 135 us (level)
  Pallas kernels: 119 us -> 116 us
  local copies, waits for them, and re-layouts: 5.61 us -> 8 us
    pallas_call x1, Pallas kernels: 31.1 us -> 25.9 us  [attention(): pl.pallas_call(functools.partial(attn_body, tq, sub, blocks, rows, scale2...]
    unnamed x9 -> x6, local copies, waits for them, and re-layouts: 2.23 us -> 6.59 us
    pallas_call x1, Pallas kernels: 52.7 us -> 54.7 us  [tail(): pl.pallas_call(functools.partial(tail_body, dims, norm), out_shape=(jax.S...]
  transfers between devices with their start and end apart: 1 -> 1, of which waited for: 0 -> 0; matrix products, arithmetic and copies ran while one was open for 0% -> 0% of each run, Pallas kernels for 23% -> 20%
where the time goes in v4:
time: 135 us; the launch traced here: 133 us
  Pallas kernels  116 us (86%)
  local copies, waits for them, and re-layouts  8 us (6%)
  starting transfers between devices  5.89 us (4%)
  other arithmetic  1.5 us (1%)
    pallas_call x1, Pallas kernels, tail(): pl.pallas_call(functools.partial(tail_body, dims, norm), out_shape=(jax.S...  54.7 us
    pallas_call x1, Pallas kernels, head(): pl.pallas_call(functools.partial(head_body, dims, q.shape[1] // k.shape[1...  35.4 us
    pallas_call x1, Pallas kernels, attention(): pl.pallas_call(functools.partial(attn_body, tq, sub, blocks, rows, scale2...  25.9 us
    unnamed x6, local copies, waits for them, and re-layouts  6.59 us
    all_to_all x1, starting transfers between devices, on_device(): lax.all_to_all(f_send, 'seq', 0, 0, tiled=True, axis_index_groups=planes)  5.89 us
  transfers between devices with their start and end apart: 1, of which 0 were waited for; matrix products, arithmetic and copies ran while one was open for 0% of the time, Pallas kernels for 20%

profile of v4, /device:TPU:1, one launch (start us, length us, event | category | flops | bytes accessed | tf_op | source)
XLA Modules:
  0.0 132.7 jit_solution(13034884319569105809)
XLA Ops:
  0.6 1.5 %pad_maximum_fusion = bf16[128,6144]{1,0:T(8,128)(2,1)S(1)} fusion(bf16[128,1024]{1,0:T(8,128)(2,1)} %bitcast.23, bf16[128,1024]{1,0:T(8,128)(2,1)} %bitcast.21, bf16[128,4096]{1,0:T(8,128)(2,1)} %bitcast.18), kind=kLoop, calls=%fused_computation.1 | loop fusion | flops 4718592 | bytes 3145728 | tf_op jit(solution)/shard_map/concatenate | solution.py:634
  2.1 1.4 %copy.16 = bf16[16,16,8,384]{3,2,0,1:T(8,128)(2,1)} copy(bf16[16,16,8,384]{3,2,1,0:T(8,128)(2,1)S(1)} %bitcast.17) | data formatting | bytes 3145728 | tf_op jit(solution)/shard_map/reshape | solution.py:637
  3.5 35.4 %head.1 = (bf16[32,128,128]{2,1,0:T(8,128)(2,1)}, bf16[32,128,128]{2,1,0:T(8,128)(2,1)}, f32[8,128]{1,0:T(8,128)}, f32[128,1024]{1,0:T(8,128)}, bf16[128,1024]{1,0:T(8,128)(2,1)}) custom-call(bf16[128,4096]{1,0:T(8,128)(2,1)} %bitcast.19, bf16[128,1024]{1,0:T(8,128)(2,1)} %bitcast.22, bf16[128,1024]{1,0:T(8,128)(2,1)} %bitcast.24, f32[1,1024]{1,0:T(1,128)} %bitcast.29, ...), custom_call_target="tpu_custom_call" | custom-call | flops 1610612736 | bytes 16777216 | tf_op jit(solution)/shard_map/head/pallas_call | solution.py:277
  38.9 5.9 %all-to-all-start = ((bf16[16,128,384]{2,1,0:T(8,128)(2,1)}), bf16[16,128,384]{2,1,0:T(8,128)(2,1)S(1)}, u32[]{:S(2)}, u32[]{:S(2)}) async-start(bf16[16,128,384]{2,1,0:T(8,128)(2,1)} %bitcast.16), calls=%async_computation | async-start | bytes 3145728 | tf_op jit(solution)/shard_map/all_to_all | solution.py:640
  45.5 25.9 %mass.1.mass_ref = f32[32,1,128]{2,1,0:T(1,128)} custom-call(s32[32]{0:T(128)} %bitcast.30, s32[1]{0:T(128)S(6)} %copy.21.limit_ref, bf16[32,128,128]{2,1,0:T(8,128)(2,1)} %get-tuple-element.15.q_hbm, bf16[32,128,128]{2,1,0:T(8,128)(2,1)} %get-tuple-element.16.k_hbm), custom_call_target="tpu_custom_call" | custom-call | flops 2147483648 | bytes 2097152 | tf_op jit(solution)/shard_map/mass/pallas_call | solution.py:118
  71.4 0.0 all-to-all-done
  71.4 0.0 copy-start
  71.4 1.2 copy-done
  72.6 54.7 %tail.1 = (f32[48,1024]{1,0:T(8,128)}, f32[8,1024]{1,0:T(8,128)}, f32[8,128]{1,0:T(8,128)}, f32[1,8]{1,0:T(1,128)}) custom-call(s32[32]{0:T(128)} %bitcast.31, s32[1]{0:T(128)S(6)} %copy.21.limit_ref, f32[32,1,128]{2,1,0:T(1,128)} %mass.1.mass_ref, f32[8,128]{1,0:T(8,128)} %get-tuple-element.18.pred_ref, bf16[8,1024]{1,0:T(8,128)(2,1)} %bitcast.27, ...), custom_call_target="tpu_custom_call" | custom-call | flops 1610612736 | bytes 8388608 | tf_op jit(solution)/shard_map/tail/pallas_call | solution.py:588
  127.3 1.6 %copy.22 = f32[48,1024]{1,0:T(8,128)} copy(f32[48,1024]{1,0:T(8,128)} %get-tuple-element.30) | data formatting | bytes 393216
  128.9 1.3 copy.23
  130.2 1.4 %copy.24 = f32[1024,8]{0,1:T(8,128)} copy(f32[1024,8]{0,1:T(8,128)} %bitcast.25) | data formatting | bytes 65536
  131.6 1.2 copy.25
Async XLA Ops:
  38.9 32.5 %all-to-all-start = ((bf16[16,128,384]{2,1,0:T(8,128)(2,1)}), bf16[16,128,384]{2,1,0:T(8,128)(2,1)S(1)}, u32[]{:S(2)}, u32[]{:S(2)}) async-start(bf16[16,128,384]{2,1,0:T(8,128)(2,1)} %bitcast.16), calls=%async_computation | async-start | bytes 3145728 | tf_op jit(solution)/shard_map/all_to_all | solution.py:640
  71.4 1.2 copy-start

commit v5 on v4

v5 whole, which is shorter than its diff:
```python
import functools
import math

import jax
import jax.numpy as jnp
from jax import lax
from jax.experimental import pallas as pl
from jax.experimental.pallas import tpu as pltpu
from jax.sharding import PartitionSpec as P

NEG = -1e30
MESH = pl.DeviceIdType.MESH


def remote(src, dst, send_sem, recv_sem, device):
    return pltpu.make_async_remote_copy(
        src_ref=src, dst_ref=dst, send_sem=send_sem, recv_sem=recv_sem, device_id=device, device_id_type=MESH
    )


def attn_core(tq, sub, total, scale2, limit, qs, ks, s_ref, acc_ref):
    lanes = 128
    groups = tq // lanes
    nt = total // tq
    eights = lambda x: x.reshape(x.shape[0] // 8, 8, tq)

    def at(j, n=tq):
        return pl.ds(pl.multiple_of(j * n, n), n)

    def scores(i, j, mx, masked):
        s = lax.dot_general(ks[at(j), :], qs[at(i), :], (((1,), (1,)), ((), ())), preferred_element_type=jnp.float32)
        if masked:
            kp = lax.broadcasted_iota(jnp.int32, (tq, tq), 0)
            qp = lax.broadcasted_iota(jnp.int32, (tq, tq), 1)
            s = jnp.where(kp <= qp, s, NEG)
        s_ref[lax.rem(i, 3), at(j), :] = s
        return jnp.maximum(mx, jnp.max(eights(s), axis=0))

    def weights(i, j, l, top):
        for u in range(tq // sub):
            here = pl.ds(pl.multiple_of(j * tq + u * sub, sub), sub)
            w = jnp.exp2((eights(s_ref[lax.rem(i, 3), here, :]) - top[None]) * scale2)
            s_ref[lax.rem(i, 3), here, :] = w.reshape(sub, tq)
            l = l + jnp.sum(w, axis=0)
        return l

    def shares(i, j, rec):
        for u in range(tq // sub):
            here = pl.ds(pl.multiple_of(j * tq + u * sub, sub), sub)
            w = (eights(s_ref[lax.rem(i, 3), here, :]) * rec[None]).reshape(sub, tq)
            tot = w[:, :lanes]
            for g in range(1, groups):
                tot = tot + w[:, g * lanes:(g + 1) * lanes]
            acc_ref[j * (tq // sub) + u] += tot

    none = jnp.full((8, tq), NEG, jnp.float32)
    zero = jnp.zeros((8, tq), jnp.float32)

    def spread_top(mx):
        return jnp.broadcast_to(jnp.max(mx, axis=0, keepdims=True), (8, tq))

    def spread_rec(i, l):
        pos = i * tq + lax.broadcasted_iota(jnp.int32, (1, tq), 1)
        rec = jnp.where(pos < limit, 1.0 / jnp.sum(l, axis=0, keepdims=True), 0.0)
        return jnp.broadcast_to(rec, (8, tq))

    def step(i, top, rec, with_scores=True, with_weights=True, with_shares=True):
        def each(j, carry):
            mx, l = carry
            if with_scores:
                mx = scores(i, j, mx, False)
            if with_weights:
                l = weights(i + 1, j, l, top)
            if with_shares:
                shares(i + 2, j, rec)
            return mx, l
        mx, l = lax.fori_loop(0, i, each, (none, zero))
        if with_scores:
            mx = scores(i, i, mx, True)
        if with_weights:
            for d in (0, 1):
                if with_scores or d:
                    l = weights(i + 1, i + d, l, top)
        if with_shares:
            for d in (0, 1, 2):
                if with_scores or with_weights and d or d == 2:
                    shares(i + 2, i + d, rec)
        return mx, l

    last = nt - 1
    mx, _ = step(last, none, none, True, False, False)
    mx, l = step(last - 1, spread_top(mx), none, True, True, False)

    def generic(t, carry):
        top, rec = carry
        i = last - t
        mx, l = step(i, top, rec)
        return spread_top(mx), spread_rec(i + 1, l)
    top, rec = lax.fori_loop(2, nt, generic, (spread_top(mx), spread_rec(last, l)))
    _, l = step(-1, top, rec, False, True, True)
    step(-2, none, spread_rec(0, l), False, False, True)


def whole_body(dims, norm, per, tq, sub, order_ref, inv_ref, limit_ref, bias_ref, q_hbm, k_hbm, v_hbm, w_hbm, bin_ref, w2t_ref, out_ref,
               feat, qa, ka, stage, wbuf, pre, pred_ref, slope_ref, act_ref, qs, ks, s_ref, acc_ref, mass_ref, f_ref,
               mrecv, lab, dl, ft, part, pair, xrecv, sm, small, smr, zs, ys, xs,
               w_sem, in_sem, i_send, i_recv, d_send, d_recv, f_send, f_recv,
               m_send, m_recv, g_send, g_recv, p_send, p_recv, x_send, x_recv, s_send, s_recv):
    ny, nz, nb = dims
    chips = ny * nz
    n = chips * 2
    s, b = lax.axis_index("seq"), lax.axis_index("batch")
    core, c = lax.rem(s, 2), s // 2
    z, y = lax.rem(c, nz), c // nz
    rows, hidden = slope_ref.shape
    head = ka.shape[2]
    q_cols, k_cols = q_hbm.shape[1], k_hbm.shape[1]
    slots, deep = wbuf.shape[:2]
    steps = w_hbm.shape[0] // deep
    chunks, tokens = len(dl), dl[0].shape[0]
    feats = part[0].shape[0]
    begin = [sum(d.shape[1] for d in dl[:j]) for j in range(chunks + 1)]
    half = feats // 2
    own_rows = half // nb
    partner = (s + 1 - 2 * core, b)

    barrier = pltpu.get_barrier_semaphore()

    def greet(r, _):
        pl.semaphore_signal(barrier, inc=1, device_id=(lax.rem(s + r, n), b), device_id_type=MESH)
        return 0
    lax.fori_loop(1, n, greet, 0)
    for r in range(1, nb):
        pl.semaphore_signal(barrier, inc=1, device_id=(s, lax.rem(b + r, nb)), device_id_type=MESH)

    inputs = []
    at = 0
    for i, ref in enumerate((q_hbm, k_hbm, v_hbm)):
        inputs.append(pltpu.make_async_copy(ref, feat.at[:, at:at + ref.shape[1]], in_sem.at[i]))
        at += ref.shape[1]
    for one in inputs:
        one.start()

    def w_copy(i):
        at = lax.rem(i, slots)
        return pltpu.make_async_copy(w_hbm.at[pl.ds(pl.multiple_of(i * deep, deep), deep), :], wbuf.at[at], w_sem.at[at])

    for i in range(slots):
        w_copy(i).start()
    acc_ref[...] = jnp.zeros_like(acc_ref)
    pre[...] = jnp.broadcast_to(bin_ref[...], pre.shape)
    for one in inputs:
        one.wait()

    def chip_at(r, sign):
        dy, dz = r // nz, lax.rem(r, nz)
        return lax.rem(y + sign * dy + ny, ny) * nz + lax.rem(z + sign * dz + nz, nz)

    def columns(i):
        return pl.ds(pl.multiple_of(i * head, head), head)

    def parts(to):
        return (columns(2 * to + core), columns(2 * to + 1 - core), columns(q_cols // head + (2 * to) // per))

    own_q, other_q, own_k = parts(c)
    qa[s] = feat[:, own_q]
    ka[s] = feat[:, own_k]
    mine = pl.ds(pl.multiple_of(c * feats, feats), feats)
    f_ref[c] = feat[:, mine]
    pl.semaphore_wait(barrier, n - 1 + nb - 1)

    def arrivals(frm):
        return (qa.at[2 * frm + core], stage.at[frm], ka.at[2 * frm + core])

    def across(i, to, frm):
        return remote(feat.at[:, parts(to)[i]], arrivals(frm)[i], i_send.at[i, to], i_recv.at[i, frm], (2 * to + core, b))

    def send(r, _):
        to = chip_at(r, 1)
        for i in (1, 2, 0):
            across(i, to, c).start()
        return 0
    lax.fori_loop(1, chips, send, 0)

    def over(i, src, at, whose):
        dst = (qa.at[2 * at + whose], ka.at[2 * at + whose])[i]
        return remote(src, dst, d_send.at[i, at], d_recv.at[i, at], partner)

    over(0, feat.at[:, other_q], c, core).start()
    over(1, feat.at[:, own_k], c, core).start()

    def step(i, _):
        w_copy(i).wait()
        x = feat[:, pl.ds(pl.multiple_of(i * deep, deep), deep)]
        pre[...] += jnp.dot(x, wbuf[lax.rem(i, slots)], preferred_element_type=jnp.float32)

        @pl.when(i + slots < steps)
        def _():
            w_copy(i + slots).start()
        return 0
    lax.fori_loop(0, steps, step, 0)
    p = pre[...]
    sig = jax.nn.sigmoid(p)
    act = (p * sig).astype(jnp.bfloat16)
    act_ref[...] = act
    slope_ref[...] = sig * (1.0 + p * (1.0 - sig))
    out = lax.dot_general(w2t_ref[...], act, (((1,), (1,)), ((), ())), preferred_element_type=jnp.float32)
    for g in range(pred_ref.shape[0]):
        pred_ref[g:g + 1, :] = out[g:g + 1, :] + bias_ref[g]

    def pass_on(r, _):
        frm = chip_at(r, -1)
        across(1, frm, frm).wait_recv()
        over(0, stage.at[frm], frm, core).start()
        across(2, frm, frm).wait_recv()
        over(1, ka.at[2 * frm + core], frm, core).start()
        return 0
    lax.fori_loop(1, chips, pass_on, 0)

    def settle(r, _):
        frm, to = chip_at(r, -1), chip_at(r, 1)
        across(0, frm, frm).wait_recv()
        for i in range(3):
            across(i, to, c).wait_send()
        return 0
    lax.fori_loop(1, chips, settle, 0)

    def settle_over(at, _):
        over(0, stage.at[at], at, 1 - core).wait()
        over(1, ka.at[2 * at + core], at, 1 - core).wait()
        return 0
    lax.fori_loop(0, chips, settle_over, 0)

    def f_copy(to, frm):
        cut = pl.ds(pl.multiple_of(to * feats, feats), feats)
        return remote(feat.at[:, cut], f_ref.at[frm], f_send.at[to], f_recv.at[frm], (2 * to + core, b))

    def f_start(r, _):
        f_copy(chip_at(r, 1), c).start()
        return 0
    lax.fori_loop(1, chips, f_start, 0)

    def sort(at, _):
        here = pl.ds(pl.multiple_of(at * rows, rows), rows)
        qs[here, :] = qa[inv_ref[at]]
        ks[here, :] = ka[inv_ref[at]]
        return 0
    lax.fori_loop(0, n, sort, 0)

    scale2 = math.log2(math.e) / math.sqrt(head)
    attn_core(tq, sub, n * rows, scale2, limit_ref[0], qs, ks, s_ref, acc_ref)

    def emit(at, _):
        block = acc_ref[order_ref[at]]
        mass_ref[at] = jnp.sum(block.T, axis=0, keepdims=True)
        return 0
    lax.fori_loop(0, n, emit, 0)

    def mass_copy(r, sender):
        to = lax.rem(s + r, n)
        return remote(mass_ref.at[to], mrecv.at[s], m_send.at[r], m_recv.at[s], (to, b))

    def mass_start(r, _):
        mass_copy(r, s).start()
        return 0
    lax.fori_loop(1, n, mass_start, 0)
    mrecv[s] = mass_ref[s]

    def f_wait(r, _):
        frm = chip_at(r, -1)
        f_copy(frm, frm).wait_recv()
        f_copy(chip_at(r, 1), c).wait_send()
        return 0
    lax.fori_loop(1, chips, f_wait, 0)
    for k in range(tokens // rows):
        ft[:, k * rows:(k + 1) * rows] = f_ref[k].T

    def mass_wait(r, _):
        frm = lax.rem(s + n - r, n)
        got = remote(mass_ref.at[frm], mrecv.at[frm], m_send.at[r], m_recv.at[frm], (frm, b))
        got.wait_recv()
        return 0
    lax.fori_loop(1, n, mass_wait, 0)

    heads = lab.shape[0]
    per = n // heads
    for g in range(heads):
        total = mrecv[per * g]
        for i in range(1, per):
            total = total + mrecv[per * g + i]
        lab[g:g + 1, :] = jnp.log1p(total)
    position = order_ref[s] * rows + lax.broadcasted_iota(jnp.int32, (1, rows), 1)
    live = jnp.where(position < limit_ref[0], 1.0, 0.0)
    resid_t = ((pred_ref[...] - lab[...]) * live * norm).astype(jnp.bfloat16)
    resid = resid_t.astype(jnp.float32).T.astype(jnp.bfloat16)
    back = jnp.dot(resid, w2t_ref[...], preferred_element_type=jnp.float32)
    delta = (back * slope_ref[...]).astype(jnp.bfloat16)
    here = pl.ds(pl.multiple_of(c * rows, rows), rows)
    for j in range(chunks):
        dl[j][here, :] = delta[:, begin[j]:begin[j + 1]]

    wide = rows // 2
    slot = {}

    def number(*key):
        return slot.setdefault(key, len(slot))

    def spot(half_id, a, e):
        return (a * nz + e) if half_id == 0 else (e * nz + a)

    def ring(v, d, size):
        return lax.rem(v + (d + size), size)

    def coords(half_id):
        return (y, z, ny, nz) if half_id == 0 else (z, y, nz, ny)

    def piece(j, block, half_id, quarter):
        r0 = half_id * wide + (quarter * (wide // 2) if quarter is not None else 0)
        size = wide // 2 if quarter is not None else wide
        return dl[j].at[pl.ds(pl.multiple_of(block * rows + r0, wide // 2), size), :]

    def neighbour(half_id, which, d):
        along_y = (half_id == 0) == (which == 0)
        to_y = ring(y, d, ny) if along_y else y
        to_z = z if along_y else ring(z, d, nz)
        return ((to_y * nz + to_z) * 2 + core, b)

    started = []

    def copy(j, half_id, which, da, de, quarter, d):
        a, e, na, ne = coords(half_id)
        block = spot(half_id, ring(a, da, na), ring(e, de, ne))
        ref = piece(j, block, half_id, quarter)
        m = number(j, half_id, which, da, de, quarter, d)
        return remote(ref, ref, g_send.at[m], g_recv.at[m], neighbour(half_id, which, d))

    def send(j, half_id, which, da, de, quarter, d):
        one = copy(j, half_id, which, da, de, quarter, d)
        one.start()
        started.append(one)

    def receive(j, half_id, which, da, de, quarter, d):
        a, e, na, ne = coords(half_id)
        back_a, back_e = (da - d, de) if which == 0 else (da, de - d)
        block = spot(half_id, ring(a, back_a, na), ring(e, back_e, ne))
        ref = piece(j, block, half_id, quarter)
        m = number(j, half_id, which, da, de, quarter, d)
        remote(ref, ref, g_send.at[m], g_recv.at[m], neighbour(half_id, which, -d)).wait_recv()

    def second(j, h, da):
        for d in (1, -1):
            send(j, h, 1, da, 0, None, d)

    def second_pass_on(j, h, da):
        receive(j, h, 1, da, 0, None, 1)
        send(j, h, 1, da, -1, 0, 1)
        receive(j, h, 1, da, 0, None, -1)
        send(j, h, 1, da, 1, 1, -1)

    def second_end(j, h, da):
        receive(j, h, 1, da, -1, 0, 1)
        receive(j, h, 1, da, 1, 1, -1)

    def stage0(j):
        for h in (0, 1):
            for d in (1, -1):
                send(j, h, 0, 0, 0, None, d)
        for h in (0, 1):
            second(j, h, 0)

    def stage1(j):
        for h in (0, 1):
            receive(j, h, 0, 0, 0, None, 1)
            send(j, h, 0, -1, 0, 0, 1)
            second(j, h, -1)
            receive(j, h, 0, 0, 0, None, -1)
            send(j, h, 0, 1, 0, 1, -1)
            second(j, h, 1)

    def stage2(j):
        for h in (0, 1):
            second_pass_on(j, h, 0)
        for h in (0, 1):
            receive(j, h, 0, -1, 0, 0, 1)
            receive(j, h, 0, 1, 0, 1, -1)
            second(j, h, 2)

    def stage3(j):
        for da in (-1, 1):
            for h in (0, 1):
                second_pass_on(j, h, da)

    def stage4(j):
        for h in (0, 1):
            second_pass_on(j, h, 2)

    def stage5(j):
        for da in (0, -1, 1, 2):
            for h in (0, 1):
                second_end(j, h, da)

    def multiply(j):
        part[j][...] = jnp.dot(ft[...], dl[j][...], preferred_element_type=jnp.float32)

    def pair_copy(j, of):
        ref = part[j].at[pl.ds(pl.multiple_of((1 - of) * half, half), half), :]
        return remote(ref, pair[j], p_send.at[j], p_recv.at[j], partner)

    def pair_start(j):
        one = pair_copy(j, core)
        one.start()
        started.append(one)

    def x_copy(j, r):
        to = lax.rem(b + r, nb)
        ref = pair[j].at[pl.ds(pl.multiple_of(to * own_rows, own_rows), own_rows), :]
        return remote(ref, xrecv[j].at[r - 1], x_send.at[j, r - 1], x_recv.at[j, r - 1], (s, to))

    def x_start(j):
        pair_copy(j, core).wait_recv()
        pair[j][...] = pair[j][...] + part[j][pl.ds(pl.multiple_of(core * half, half), half), :]
        for r in (2, 1, 3)[: nb - 1]:
            one = x_copy(j, r)
            one.start()
            started.append(one)

    def x_end(j):
        for r in range(1, nb):
            x_copy(j, r).wait_recv()
        own = pair[j][pl.ds(pl.multiple_of(b * own_rows, own_rows), own_rows), :]
        for r in range(1, nb):
            own = own + xrecv[j][r - 1]
        out_ref[:own_rows, begin[j]:begin[j + 1]] = own

    def small_start0():
        sw = sm.shape[2]
        out_term = jnp.dot(resid_t, act_ref[...], preferred_element_type=jnp.float32)
        sums = jnp.sum(delta.astype(jnp.float32), axis=0, keepdims=True)
        bias = jnp.sum(resid.astype(jnp.float32), axis=0, keepdims=True)
        lanes = 128
        cols = [out_term[:, k * lanes:(k + 1) * lanes] for k in range(hidden // lanes)]
        cols.append(jnp.concatenate([sums[:, k * lanes:(k + 1) * lanes] for k in range(hidden // lanes)], axis=0))
        cols.append(jnp.zeros((heads, lanes), jnp.float32))
        each = sw // lanes
        for k, value in enumerate(cols):
            sm[k // each, :, (k % each) * lanes:(k % each + 1) * lanes] = value
        at = (len(cols) - 1) % each * lanes
        sm[1, 0:1, at:at + heads] = bias
        one = remote(sm.at[1 - core], smr, s_send.at[0], s_recv.at[0], partner)
        one.start()
        started.append(one)

    def small_hop(level, value, buf, at, size, target):
        buf[at] = value
        for r in range(1, size):
            one = remote(buf.at[at], buf.at[at], s_send.at[level * 3 + r], s_recv.at[level * 3 + r], target(r))
            one.start()
            started.append(one)

    def small_sum(level, buf, at, size, target):
        for r in range(1, size):
            frm = lax.rem(at + size - r, size)
            remote(buf.at[frm], buf.at[frm], s_send.at[level * 3 + r], s_recv.at[level * 3 + r], target(r)).wait_recv()
        total = buf[0]
        for k in range(1, size):
            total = total + buf[k]
        return total

    to_z = lambda r: ((y * nz + lax.rem(z + r, nz)) * 2 + core, b)
    to_y = lambda r: ((lax.rem(y + r, ny) * nz + z) * 2 + core, b)
    to_x = lambda r: (s, lax.rem(b + r, nb))

    def small1():
        remote(sm.at[1 - core], smr, s_send.at[0], s_recv.at[0], partner).wait_recv()
        small_hop(0, sm[core] + smr[...], zs, z, nz, to_z)

    def small2():
        small_hop(1, small_sum(0, zs, z, nz, to_z), ys, y, ny, to_y)

    def small3():
        small_hop(2, small_sum(1, ys, y, ny, to_y), xs, b, nb, to_x)

    def small4():
        sm[core] = small_sum(2, xs, b, nb, to_x)
        one = remote(sm.at[core], small.at[core], s_send.at[10], s_recv.at[10], partner)
        one.start()
        started.append(one)
        small[core] = sm[core]

    def small5():
        remote(sm.at[1 - core], small.at[1 - core], s_send.at[10], s_recv.at[10], partner).wait_recv()
        sw = small.shape[2]
        out_ref[own_rows:own_rows + heads, :sw] = small[0]
        out_ref[own_rows:own_rows + heads, sw:] = small[1, :, :hidden - sw]
        base = own_rows + heads
        lanes = 128
        for k in range(hidden // lanes):
            out_ref[base:base + 1, k * lanes:(k + 1) * lanes] = small[1, k:k + 1, hidden - sw:hidden - sw + lanes]
        out_ref[base + 1:base + 2, :lanes] = small[1, 0:1, hidden - sw + lanes:hidden - sw + 2 * lanes]

    stage0(0); small_start0(); stage1(0); stage2(0); stage0(1); stage3(0); small1(); stage1(1); stage4(0)
    stage2(1); stage5(0); small2(); stage3(1)
    multiply(0); pair_start(0); stage4(1); small3()
    x_start(0); stage5(1)
    multiply(1); pair_start(1); small4(); x_end(0); x_start(1); small5(); x_end(1)

    for one in started:
        one.wait_send()

    def mass_drain(r, _):
        mass_copy(r, s).wait_send()
        return 0
    lax.fori_loop(1, n, mass_drain, 0)


def whole(dims, norm, order, inverse, limit, bias, q, k, v, w_in, b_in, w2t, tq=512, sub=128, widths=(640, 384), slots=3, deep=512):
    ny, nz, nb = dims
    rows, hidden = q.shape[0], w_in.shape[1]
    heads = w2t.shape[0]
    size = k.shape[1] // heads
    chips = ny * nz
    n = 2 * chips
    tokens = chips * rows
    columns = w_in.shape[0]
    feats = columns // chips
    half = feats // 2
    chunks = len(widths)
    sw = (hidden + 256) // 2
    vm, dma = pltpu.VMEM, pltpu.SemaphoreType.DMA
    block = lambda space: pl.BlockSpec(memory_space=space)
    f32, bf16 = jnp.float32, jnp.bfloat16
    return pl.pallas_call(
        functools.partial(whole_body, dims, norm, q.shape[1] // k.shape[1], tq, sub),
        out_shape=jax.ShapeDtypeStruct((half // nb + 16, hidden), f32),
        in_specs=[block(pltpu.SMEM)] * 4 + [block(pltpu.HBM)] * 4 + [block(vm)] * 2,
        out_specs=block(vm),
        scratch_shapes=[
            vm((rows, columns), bf16),
            vm((n, rows, size), bf16),
            vm((n, rows, size), bf16),
            vm((chips, rows, size), bf16),
            vm((slots, deep, hidden), bf16),
            vm((rows, hidden), f32),
            vm((heads, rows), f32),
            vm((rows, hidden), f32),
            vm((rows, hidden), bf16),
            vm((n * rows, size), bf16),
            vm((n * rows, size), bf16),
            vm((3, n * rows, tq), f32),
            vm((n, rows, 128), f32),
            vm((n, 1, rows), f32),
            vm((chips, rows, feats), bf16),
            vm((n, 1, rows), f32),
            vm((heads, rows), f32),
            tuple(vm((tokens, w), bf16) for w in widths),
            vm((feats, tokens), bf16),
            tuple(vm((feats, w), f32) for w in widths),
            tuple(vm((half, w), f32) for w in widths),
            tuple(vm((nb - 1, half // nb, w), f32) for w in widths),
            vm((2, heads, sw), f32),
            vm((2, heads, sw), f32),
            vm((heads, sw), f32),
            vm((nz, heads, sw), f32),
            vm((ny, heads, sw), f32),
            vm((nb, heads, sw), f32),
            dma((slots,)), dma((3,)),
            dma((3, chips)), dma((3, chips)),
            dma((2, chips)), dma((2, chips)),
            dma((chips,)), dma((chips,)),
            dma((n,)), dma((n,)),
            dma((chunks * 40,)), dma((chunks * 40,)),
            dma((chunks,)), dma((chunks,)),
            dma((chunks, nb - 1)), dma((chunks, nb - 1)),
            dma((12,)), dma((12,)),
        ],
        compiler_params=pltpu.CompilerParams(collective_id=1, has_side_effects=True, vmem_limit_bytes=60 * 2**20),
        name="whole",
    )(order, inverse, limit, bias, q, k, v, w_in, b_in, w2t)


def on_device(dims, queries, keys, values, lengths, block_pos, w_in, b_in, output_weight, output_bias):
    hidden, heads = output_weight.shape
    total = lax.axis_size("seq") * queries.shape[1]
    norm = 1.0 / math.sqrt(lax.axis_size("batch") * total)
    order = block_pos[0]
    stored = jnp.arange(order.shape[0], dtype=jnp.int32)
    inverse = jnp.sum(jnp.where(order[None, :] == stored[:, None], stored[None, :], 0), axis=1)
    out = whole(
        dims, norm, order, inverse, lengths, output_bias, queries[0], keys[0], values[0], w_in, b_in[None, :], output_weight.T
    )
    own = out.shape[0] - 16
    return (out[:own], out[own + heads], out[own:own + heads].T, out[own + heads + 1, :heads])


def solution(mesh):
    nb = mesh.shape["batch"]
    ny = nz = math.isqrt(mesh.shape["seq"] // 2)
    return jax.shard_map(
        functools.partial(on_device, (ny, nz, nb)),
        mesh=mesh,
        in_specs=(
            P("batch", "seq", None),
            P("batch", "seq", None),
            P("batch", "seq", None),
            P("batch"),
            P("batch", None),
            P(),
            P(),
            P(),
            P(),
        ),
        out_specs=(P(("seq", "batch"), None), P(), P(), P()),
        check_vma=False,
    )
```

time: 135 us -> 116 us (0.86)
  Pallas kernels: 116 us -> 106 us
  starting transfers between devices: 5.89 us -> 0 us
  local copies, waits for them, and re-layouts: 8 us -> 5.53 us
    pallas_call x3 -> x1, Pallas kernels: 116 us -> 106 us  [whole(): pl.pallas_call(functools.partial(whole_body, dims, norm, q.shape[1] // k....]
    unnamed x6 -> x0, local copies, waits for them, and re-layouts: 6.59 us -> none
    all_to_all x1 -> x0, starting transfers between devices: 5.89 us -> none  [on_device(): lax.all_to_all(f_send, 'seq', 0, 0, tiled=True, axis_index_groups=planes)]
    slice x0 -> x2, local copies, waits for them, and re-layouts: none -> 2.97 us  [the longest x1 1.62 us: on_device(): out[:own]]
    concatenate x1 -> x0, other arithmetic: 1.5 us -> none  [on_device(): features = jnp.concatenate([q_rows, k_rows, v_rows], axis=1)]
    reshape x1 -> x0, local copies, waits for them, and re-layouts: 1.41 us -> none  [on_device(): f_send = features.reshape(rows, chips, cols).transpose(1, 0, 2)]
    transpose x0 -> x1, local copies, waits for them, and re-layouts: none -> 1.37 us  [on_device(): out[own:own + heads]]
  transfers between devices with their start and end apart: 1 -> 0, of which waited for: 0 -> 0; matrix products, arithmetic and copies ran while one was open for 0% -> 0% of each run, Pallas kernels for 20% -> 0%
where the time goes in v5:
time: 116 us; the launch traced here: 114 us
  Pallas kernels  106 us (91%)
  local copies, waits for them, and re-layouts  5.53 us (5%)
  between operations  1.29 us (1%)
  other arithmetic  1.28 us (1%)
    pallas_call x1, Pallas kernels, whole(): pl.pallas_call(functools.partial(whole_body, dims, norm, q.shape[1] // k....  106 us

profile of v5, /device:TPU:1, one launch (start us, length us, event | category | flops | bytes accessed | tf_op | source)
XLA Modules:
  0.0 114.2 jit_solution(12747745120693202840)
XLA Ops:
  1.3 1.3 %select_reduce_fusion.inv_ref = s32[32]{0:T(128)} fusion(s32[32]{0:T(128)} %bitcast.17), kind=kLoop, calls=%fused_computation.1 | loop fusion | flops 3040 | bytes 256 | tf_op jit(solution)/shard_map/reduce_sum | solution.py:587
  2.6 106.1 %whole.1 = f32[64,1024]{1,0:T(8,128)} custom-call(s32[32]{0:T(128)} %bitcast.18, s32[32]{0:T(128)} %select_reduce_fusion.inv_ref, s32[1]{0:T(128)S(6)} %copy.13.limit_ref, f32[8]{0:T(128)} %bias_ref.1, bf16[128,4096]{1,0:T(8,128)(2,1)} %bitcast.11, bf16[128,1024]{1,0:T(8,128)(2,1)} %bitcast.12, bf16[128,1024]{1,0:T(8,128)(2,1)} %bitcast.13, ...), custom_call_target="tpu_custom_call" | custom-call | tf_op jit(solution)/shard_map/whole/pallas_call | solution.py:532
  108.6 1.2 %slice_bitcast_fusion.1 = f32[8]{0:T(128)} fusion(f32[64,1024]{1,0:T(8,128)} %whole.1), kind=kLoop, calls=%fused_computation.3 | loop fusion | bytes 64 | tf_op jit(solution)/shard_map/squeeze | solution.py:592
  109.8 1.4 %slice.13 = f32[1,1024]{1,0:T(1,128)} slice(f32[64,1024]{1,0:T(8,128)} %whole.1), slice={[56:57], [0:1024]} | slice | bytes 8192 | tf_op jit(solution)/shard_map/slice | solution.py:592
  111.2 1.4 %slice_bitcast_fusion = f32[1024,8]{0,1:T(8,128)} fusion(f32[64,1024]{1,0:T(8,128)} %whole.1), kind=kLoop, calls=%fused_computation | loop fusion | bytes 65536 | tf_op jit(solution)/shard_map/transpose | solution.py:592
  112.6 1.6 %slice.12 = f32[48,1024]{1,0:T(8,128)} slice(f32[64,1024]{1,0:T(8,128)} %whole.1), slice={[0:48], [0:1024]} | slice | bytes 393216 | tf_op jit(solution)/shard_map/slice | solution.py:592

commit v6 on v5

--- a/solution.py
+++ b/solution.py
@@ -18,7 +18,7 @@
     )
 
 
-def attn_core(tq, sub, total, scale2, limit, qs, ks, s_ref, acc_ref):
+def attn_core(tq, sub, total, scale2, limit, qs, ks, bufs, acc_ref, done=None):
     lanes = 128
     groups = tq // lanes
     nt = total // tq
@@ -33,29 +33,28 @@
             kp = lax.broadcasted_iota(jnp.int32, (tq, tq), 0)
             qp = lax.broadcasted_iota(jnp.int32, (tq, tq), 1)
             s = jnp.where(kp <= qp, s, NEG)
-        s_ref[lax.rem(i, 3), at(j), :] = s
+        bufs[i % 3][at(j), :] = s
         return jnp.maximum(mx, jnp.max(eights(s), axis=0))
 
     def weights(i, j, l, top):
+        buf = bufs[i % 3]
         for u in range(tq // sub):
             here = pl.ds(pl.multiple_of(j * tq + u * sub, sub), sub)
-            w = jnp.exp2((eights(s_ref[lax.rem(i, 3), here, :]) - top[None]) * scale2)
-            s_ref[lax.rem(i, 3), here, :] = w.reshape(sub, tq)
+            w = jnp.exp2((eights(buf[here, :]) - top[None]) * scale2)
+            buf[here, :] = w.reshape(sub, tq)
             l = l + jnp.sum(w, axis=0)
         return l
 
     def shares(i, j, rec):
+        buf = bufs[i % 3]
         for u in range(tq // sub):
             here = pl.ds(pl.multiple_of(j * tq + u * sub, sub), sub)
-            w = (eights(s_ref[lax.rem(i, 3), here, :]) * rec[None]).reshape(sub, tq)
+            w = (eights(buf[here, :]) * rec[None]).reshape(sub, tq)
             tot = w[:, :lanes]
             for g in range(1, groups):
                 tot = tot + w[:, g * lanes:(g + 1) * lanes]
             acc_ref[j * (tq // sub) + u] += tot
 
-    none = jnp.full((8, tq), NEG, jnp.float32)
-    zero = jnp.zeros((8, tq), jnp.float32)
-
     def spread_top(mx):
         return jnp.broadcast_to(jnp.max(mx, axis=0, keepdims=True), (8, tq))
 
@@ -64,45 +63,38 @@
         rec = jnp.where(pos < limit, 1.0 / jnp.sum(l, axis=0, keepdims=True), 0.0)
         return jnp.broadcast_to(rec, (8, tq))
 
-    def step(i, top, rec, with_scores=True, with_weights=True, with_shares=True):
-        def each(j, carry):
+    top = rec = None
+    for i in range(nt - 1, -3, -1):
+        first, second, third = i >= 0, 0 <= i + 1 < nt, i + 2 < nt
+
+        def each(j, carry, i=i, first=first, second=second, third=third, top=top, rec=rec):
             mx, l = carry
-            if with_scores:
+            if first:
                 mx = scores(i, j, mx, False)
-            if with_weights:
+            if second:
                 l = weights(i + 1, j, l, top)
-            if with_shares:
+            if third:
                 shares(i + 2, j, rec)
             return mx, l
-        mx, l = lax.fori_loop(0, i, each, (none, zero))
-        if with_scores:
+
+        mx = jnp.full((8, tq), NEG, jnp.float32)
+        l = jnp.zeros((8, tq), jnp.float32)
+        if i > 0:
+            mx, l = lax.fori_loop(0, i, each, (mx, l))
+        if first:
             mx = scores(i, i, mx, True)
-        if with_weights:
-            for d in (0, 1):
-                if with_scores or d:
-                    l = weights(i + 1, i + d, l, top)
-        if with_shares:
-            for d in (0, 1, 2):
-                if with_scores or with_weights and d or d == 2:
-                    shares(i + 2, i + d, rec)
-        return mx, l
-
-    last = nt - 1
-    mx, _ = step(last, none, none, True, False, False)
-    mx, l = step(last - 1, spread_top(mx), none, True, True, False)
-
-    def generic(t, carry):
-        top, rec = carry
-        i = last - t
-        mx, l = step(i, top, rec)
-        return spread_top(mx), spread_rec(i + 1, l)
-    top, rec = lax.fori_loop(2, nt, generic, (spread_top(mx), spread_rec(last, l)))
-    _, l = step(-1, top, rec, False, True, True)
-    step(-2, none, spread_rec(0, l), False, False, True)
+        for d in (0, 1, 2):
+            if second and d < 2 and i + d >= 0:
+                l = weights(i + 1, i + d, l, top)
+            if third and i + d >= 0:
+                shares(i + 2, i + d, rec)
+        if third and done is not None:
+            done(i + 2)
+        top, rec = spread_top(mx), spread_rec(i + 1, l)
 
 
 def whole_body(dims, norm, per, tq, sub, order_ref, inv_ref, limit_ref, bias_ref, q_hbm, k_hbm, v_hbm, w_hbm, bin_ref, w2t_ref, out_ref,
-               feat, qa, ka, stage, wbuf, pre, pred_ref, slope_ref, act_ref, qs, ks, s_ref, acc_ref, mass_ref, f_ref,
+               feat, qa, ka, stage, wbuf, pre, pred_ref, slope_ref, act_ref, qs, ks, bufs, acc_ref, msort, mass_ref, f_ref,
                mrecv, lab, dl, ft, part, pair, xrecv, sm, small, smr, zs, ys, xs,
                w_sem, in_sem, i_send, i_recv, d_send, d_recv, f_send, f_recv,
                m_send, m_recv, g_send, g_recv, p_send, p_recv, x_send, x_recv, s_send, s_recv):
@@ -152,8 +144,11 @@
     for one in inputs:
         one.wait()
 
-    def chip_at(r, sign):
-        dy, dz = r // nz, lax.rem(r, nz)
+    hops = lambda d: -min(d[0], ny - d[0]) - min(d[1], nz - d[1])
+    away = sorted(((dy, dz) for dy in range(ny) for dz in range(nz) if dy or dz), key=hops)
+
+    def chip_at(d, sign):
+        dy, dz = d
         return lax.rem(y + sign * dy + ny, ny) * nz + lax.rem(z + sign * dz + nz, nz)
 
     def columns(i):
@@ -175,12 +170,10 @@
     def across(i, to, frm):
         return remote(feat.at[:, parts(to)[i]], arrivals(frm)[i], i_send.at[i, to], i_recv.at[i, frm], (2 * to + core, b))
 
-    def send(r, _):
-        to = chip_at(r, 1)
-        for i in (1, 2, 0):
-            across(i, to, c).start()
-        return 0
-    lax.fori_loop(1, chips, send, 0)
+    for some in ((1, 2), (0,)):
+        for d in away:
+            for i in some:
+                across(i, chip_at(d, 1), c).start()
 
     def over(i, src, at, whose):
         dst = (qa.at[2 * at + whose], ka.at[2 * at + whose])[i]
@@ -208,20 +201,20 @@
     for g in range(pred_ref.shape[0]):
         pred_ref[g:g + 1, :] = out[g:g + 1, :] + bias_ref[g]
 
-    def pass_on(r, _):
-        frm = chip_at(r, -1)
+    for d in away:
+        frm = chip_at(d, -1)
         across(1, frm, frm).wait_recv()
         over(0, stage.at[frm], frm, core).start()
         across(2, frm, frm).wait_recv()
         over(1, ka.at[2 * frm + core], frm, core).start()
-        return 0
-    lax.fori_loop(1, chips, pass_on, 0)
+
+    def all_others(r):
+        return lax.rem(c + r, chips)
 
     def settle(r, _):
-        frm, to = chip_at(r, -1), chip_at(r, 1)
-        across(0, frm, frm).wait_recv()
+        across(0, all_others(r), all_others(r)).wait_recv()
         for i in range(3):
-            across(i, to, c).wait_send()
+            across(i, all_others(r), c).wait_send()
         return 0
     lax.fori_loop(1, chips, settle, 0)
 
@@ -235,10 +228,8 @@
         cut = pl.ds(pl.multiple_of(to * feats, feats), feats)
         return remote(feat.at[:, cut], f_ref.at[frm], f_send.at[to], f_recv.at[frm], (2 * to + core, b))
 
-    def f_start(r, _):
-        f_copy(chip_at(r, 1), c).start()
-        return 0
-    lax.fori_loop(1, chips, f_start, 0)
+    for d in away:
+        f_copy(chip_at(d, 1), c).start()
 
     def sort(at, _):
         here = pl.ds(pl.multiple_of(at * rows, rows), rows)
@@ -248,11 +239,15 @@
     lax.fori_loop(0, n, sort, 0)
 
     scale2 = math.log2(math.e) / math.sqrt(head)
-    attn_core(tq, sub, n * rows, scale2, limit_ref[0], qs, ks, s_ref, acc_ref)
+
+    def done(i):
+        for u in range(i * (tq // rows), (i + 1) * (tq // rows)):
+            msort[u] = jnp.sum(acc_ref[u].T, axis=0, keepdims=True)
+
+    attn_core(tq, sub, n * rows, scale2, limit_ref[0], qs, ks, bufs, acc_ref, done)
 
     def emit(at, _):
-        block = acc_ref[order_ref[at]]
-        mass_ref[at] = jnp.sum(block.T, axis=0, keepdims=True)
+        mass_ref[at] = msort[order_ref[at]]
         return 0
     lax.fori_loop(0, n, emit, 0)
 
@@ -267,9 +262,8 @@
     mrecv[s] = mass_ref[s]
 
     def f_wait(r, _):
-        frm = chip_at(r, -1)
-        f_copy(frm, frm).wait_recv()
-        f_copy(chip_at(r, 1), c).wait_send()
+        f_copy(all_others(r), all_others(r)).wait_recv()
+        f_copy(all_others(r), c).wait_send()
         return 0
     lax.fori_loop(1, chips, f_wait, 0)
     for k in range(tokens // rows):
@@ -498,11 +492,32 @@
             out_ref[base:base + 1, k * lanes:(k + 1) * lanes] = small[1, k:k + 1, hidden - sw:hidden - sw + lanes]
         out_ref[base + 1:base + 2, :lanes] = small[1, 0:1, hidden - sw + lanes:hidden - sw + 2 * lanes]
 
-    stage0(0); small_start0(); stage1(0); stage2(0); stage0(1); stage3(0); small1(); stage1(1); stage4(0)
-    stage2(1); stage5(0); small2(); stage3(1)
-    multiply(0); pair_start(0); stage4(1); small3()
-    x_start(0); stage5(1)
-    multiply(1); pair_start(1); small4(); x_end(0); x_start(1); small5(); x_end(1)
+    stage0(0)
+    stage0(1)
+    small_start0()
+    stage1(0)
+    stage2(0)
+    stage1(1)
+    small1()
+    stage3(0)
+    stage2(1)
+    stage4(0)
+    small2()
+    stage3(1)
+    stage5(0)
+    multiply(0)
+    pair_start(0)
+    stage4(1)
+    small3()
+    x_start(0)
+    stage5(1)
+    multiply(1)
+    pair_start(1)
+    small4()
+    x_start(1)
+    x_end(0)
+    small5()
+    x_end(1)
 
     for one in started:
         one.wait_send()
@@ -513,7 +528,7 @@
     lax.fori_loop(1, n, mass_drain, 0)
 
 
-def whole(dims, norm, order, inverse, limit, bias, q, k, v, w_in, b_in, w2t, tq=512, sub=128, widths=(640, 384), slots=3, deep=512):
+def whole(dims, norm, order, inverse, limit, bias, q, k, v, w_in, b_in, w2t, tq=512, sub=128, widths=(512, 512), slots=3, deep=512):
     ny, nz, nb = dims
     rows, hidden = q.shape[0], w_in.shape[1]
     heads = w2t.shape[0]
@@ -546,8 +561,9 @@
             vm((rows, hidden), bf16),
             vm((n * rows, size), bf16),
             vm((n * rows, size), bf16),
-            vm((3, n * rows, tq), f32),
+            tuple(vm((n * rows, tq), f32) for _ in range(3)),
             vm((n, rows, 128), f32),
+            vm((n, 1, rows), f32),
             vm((n, 1, rows), f32),
             vm((chips, rows, feats), bf16),
             vm((n, 1, rows), f32),
@@ -578,6 +594,25 @@
     )(order, inverse, limit, bias, q, k, v, w_in, b_in, w2t)
 
 
+def apart_body(own, heads, out_ref, grad_ref, ow_ref, gb_ref, bias_ref):
+    grad_ref[...] = out_ref[:own]
+    ow_ref[...] = out_ref[own:own + heads]
+    gb_ref[...] = out_ref[own + heads:own + heads + 1]
+    bias_ref[...] = out_ref[own + heads + 1:own + heads + 2, :heads]
+
+
+def apart(own, heads, out):
+    hidden = out.shape[1]
+    shapes = ((own, hidden), (heads, hidden), (1, hidden), (1, heads))
+    return pl.pallas_call(
+        functools.partial(apart_body, own, heads),
+        out_shape=tuple(jax.ShapeDtypeStruct(one, jnp.float32) for one in shapes),
+        in_specs=[pl.BlockSpec(memory_space=pltpu.VMEM)],
+        out_specs=[pl.BlockSpec(memory_space=pltpu.VMEM)] * 4,
+        name="apart",
+    )(out)
+
+
 def on_device(dims, queries, keys, values, lengths, block_pos, w_in, b_in, output_weight, output_bias):
     hidden, heads = output_weight.shape
     total = lax.axis_size("seq") * queries.shape[1]
@@ -589,7 +624,8 @@
         dims, norm, order, inverse, lengths, output_bias, queries[0], keys[0], values[0], w_in, b_in[None, :], output_weight.T
     )
     own = out.shape[0] - 16
-    return (out[:own], out[own + heads], out[own:own + heads].T, out[own + heads + 1, :heads])
+    grad, ow, gb, bias = apart(own, heads, out)
+    return (grad, gb.reshape(hidden), ow.T, bias.reshape(heads))
 
 
 def solution(mesh):

time: 116 us -> 102 us (0.88)
  Pallas kernels: 106 us -> 98.7 us
  local copies, waits for them, and re-layouts: 5.53 us -> 0 us
    pallas_call x1, Pallas kernels: 106 us -> 97.1 us  [whole(): pl.pallas_call(functools.partial(whole_body, dims, norm, q.shape[1] // k....]
    slice x2 -> x0, local copies, waits for them, and re-layouts: 2.97 us -> none  [the longest x1 1.62 us: on_device(): out[:own]]
    pallas_call x0 -> x1, Pallas kernels: none -> 1.65 us  [apart(): pl.pallas_call(functools.partial(apart_body, own, heads), out_shape=tuple...]
    transpose x1 -> x0, local copies, waits for them, and re-layouts: 1.37 us -> none  [on_device(): out[own:own + heads]]
    squeeze x1 -> x0, local copies, waits for them, and re-layouts: 1.19 us -> none  [on_device(): out[own + heads + 1, :heads]]
where the time goes in v6:
time: 102 us; the launch traced here: 101 us
  Pallas kernels  98.7 us (97%)
  between operations  1.29 us (1%)
  other arithmetic  1.28 us (1%)
    pallas_call x1, Pallas kernels, whole(): pl.pallas_call(functools.partial(whole_body, dims, norm, q.shape[1] // k....  97.1 us

profile of v6, /device:TPU:1, one launch (start us, length us, event | category | flops | bytes accessed | tf_op | source)
XLA Modules:
  0.0 101.3 jit_solution(15642300384231506189)
XLA Ops:
  1.3 1.3 %select_reduce_fusion.inv_ref = s32[32]{0:T(128)} fusion(s32[32]{0:T(128)} %bitcast.14), kind=kLoop, calls=%fused_computation | loop fusion | flops 3040 | bytes 256 | tf_op jit(solution)/shard_map/reduce_sum | solution.py:622
  2.6 97.1 %whole.1.out_ref = f32[64,1024]{1,0:T(8,128)} custom-call(s32[32]{0:T(128)} %bitcast.15, s32[32]{0:T(128)} %select_reduce_fusion.inv_ref, s32[1]{0:T(128)S(6)} %copy.13.limit_ref, f32[8]{0:T(128)} %bias_ref.1, bf16[128,4096]{1,0:T(8,128)(2,1)} %bitcast.9, bf16[128,1024]{1,0:T(8,128)(2,1)} %bitcast.10, bf16[128,1024]{1,0:T(8,128)(2,1)} %bitcast.11, ...), custom_call_target="tpu_custom_call" | custom-call | tf_op jit(solution)/shard_map/whole/pallas_call | solution.py:547
  99.6 1.6 %apart.1 = (f32[48,1024]{1,0:T(8,128)}, f32[8,1024]{1,0:T(8,128)}, f32[1,1024]{1,0:T(1,128)}, f32[1,8]{1,0:T(1,128)}) custom-call(f32[64,1024]{1,0:T(8,128)} %whole.1.out_ref), custom_call_target="tpu_custom_call" | custom-call | tf_op jit(solution)/shard_map/apart/pallas_call | solution.py:607

commit v7 on v6

--- a/solution.py
+++ b/solution.py
@@ -93,7 +93,7 @@
         top, rec = spread_top(mx), spread_rec(i + 1, l)
 
 
-def whole_body(dims, norm, per, tq, sub, order_ref, inv_ref, limit_ref, bias_ref, q_hbm, k_hbm, v_hbm, w_hbm, bin_ref, w2t_ref, out_ref,
+def whole_body(dims, norm, per, tq, sub, order_ref, bias_ref, limit_ref, q_hbm, k_hbm, v_hbm, w_hbm, bin_ref, w2t_ref, out_ref,
                feat, qa, ka, stage, wbuf, pre, pred_ref, slope_ref, act_ref, qs, ks, bufs, acc_ref, msort, mass_ref, f_ref,
                mrecv, lab, dl, ft, part, pair, xrecv, sm, small, smr, zs, ys, xs,
                w_sem, in_sem, i_send, i_recv, d_send, d_recv, f_send, f_recv,
@@ -232,9 +232,13 @@
         f_copy(chip_at(d, 1), c).start()
 
     def sort(at, _):
+        stored = jnp.int32(0)
+        for k in range(1, n):
+            stored = stored + k * jnp.maximum(1 - jnp.abs(order_ref[k] - at), 0)
         here = pl.ds(pl.multiple_of(at * rows, rows), rows)
-        qs[here, :] = qa[inv_ref[at]]
-        ks[here, :] = ka[inv_ref[at]]
+        stored = jnp.minimum(stored, n - 1)
+        qs[here, :] = qa[stored]
+        ks[here, :] = ka[stored]
         return 0
     lax.fori_loop(0, n, sort, 0)
 
@@ -244,7 +248,7 @@
         for u in range(i * (tq // rows), (i + 1) * (tq // rows)):
             msort[u] = jnp.sum(acc_ref[u].T, axis=0, keepdims=True)
 
-    attn_core(tq, sub, n * rows, scale2, limit_ref[0], qs, ks, bufs, acc_ref, done)
+    attn_core(tq, sub, n * rows, scale2, limit_ref[...], qs, ks, bufs, acc_ref, done)
 
     def emit(at, _):
         mass_ref[at] = msort[order_ref[at]]
@@ -284,7 +288,7 @@
             total = total + mrecv[per * g + i]
         lab[g:g + 1, :] = jnp.log1p(total)
     position = order_ref[s] * rows + lax.broadcasted_iota(jnp.int32, (1, rows), 1)
-    live = jnp.where(position < limit_ref[0], 1.0, 0.0)
+    live = jnp.where(position < limit_ref[...], 1.0, 0.0)
     resid_t = ((pred_ref[...] - lab[...]) * live * norm).astype(jnp.bfloat16)
     resid = resid_t.astype(jnp.float32).T.astype(jnp.bfloat16)
     back = jnp.dot(resid, w2t_ref[...], preferred_element_type=jnp.float32)
@@ -528,7 +532,7 @@
     lax.fori_loop(1, n, mass_drain, 0)
 
 
-def whole(dims, norm, order, inverse, limit, bias, q, k, v, w_in, b_in, w2t, tq=512, sub=128, widths=(512, 512), slots=3, deep=512):
+def whole(dims, norm, order, bias, limit, q, k, v, w_in, b_in, w2t, tq=512, sub=128, widths=(512, 512), slots=3, deep=512):
     ny, nz, nb = dims
     rows, hidden = q.shape[0], w_in.shape[1]
     heads = w2t.shape[0]
@@ -547,7 +551,7 @@
     return pl.pallas_call(
         functools.partial(whole_body, dims, norm, q.shape[1] // k.shape[1], tq, sub),
         out_shape=jax.ShapeDtypeStruct((half // nb + 16, hidden), f32),
-        in_specs=[block(pltpu.SMEM)] * 4 + [block(pltpu.HBM)] * 4 + [block(vm)] * 2,
+        in_specs=[block(pltpu.SMEM)] * 2 + [block(vm)] + [block(pltpu.HBM)] * 4 + [block(vm)] * 2,
         out_specs=block(vm),
         scratch_shapes=[
             vm((rows, columns), bf16),
@@ -591,7 +595,7 @@
         ],
         compiler_params=pltpu.CompilerParams(collective_id=1, has_side_effects=True, vmem_limit_bytes=60 * 2**20),
         name="whole",
-    )(order, inverse, limit, bias, q, k, v, w_in, b_in, w2t)
+    )(order, bias, limit, q, k, v, w_in, b_in, w2t)
 
 
 def apart_body(own, heads, out_ref, grad_ref, ow_ref, gb_ref, bias_ref):
@@ -617,11 +621,8 @@
     hidden, heads = output_weight.shape
     total = lax.axis_size("seq") * queries.shape[1]
     norm = 1.0 / math.sqrt(lax.axis_size("batch") * total)
-    order = block_pos[0]
-    stored = jnp.arange(order.shape[0], dtype=jnp.int32)
-    inverse = jnp.sum(jnp.where(order[None, :] == stored[:, None], stored[None, :], 0), axis=1)
     out = whole(
-        dims, norm, order, inverse, lengths, output_bias, queries[0], keys[0], values[0], w_in, b_in[None, :], output_weight.T
+        dims, norm, block_pos[0], output_bias, lengths[None, :], queries[0], keys[0], values[0], w_in, b_in[None, :], output_weight.T
     )
     own = out.shape[0] - 16
     grad, ow, gb, bias = apart(own, heads, out)

time: 102 us -> 100 us (0.980)
  other arithmetic: 1.28 us -> 0 us
    reduce_sum x1 -> x0, other arithmetic: 1.28 us -> none  [on_device(): jnp.sum(jnp.where(order[None, :] == stored[:, None], stored[None, :], 0),...]
where the time goes in v7:
time: 100 us
  Pallas kernels  98.8 us (99%)
  between operations  1.29 us (1%)
    pallas_call x1, Pallas kernels, whole(): pl.pallas_call(functools.partial(whole_body, dims, norm, q.shape[1] // k....  97.2 us

profile of v7, /device:TPU:1, one launch (start us, length us, event | category | flops | bytes accessed | tf_op | source)
XLA Modules:
  0.0 100.1 jit_solution(3853591935031215465)
XLA Ops:
  1.3 97.2 %whole.1.out_ref = f32[64,1024]{1,0:T(8,128)} custom-call(s32[32]{0:T(128)} %bitcast.16, f32[8]{0:T(128)} %bias_ref.1, s32[1,1]{1,0:T(1,128)} %bitcast.10.limit_ref, bf16[128,4096]{1,0:T(8,128)(2,1)} %bitcast.11, bf16[128,1024]{1,0:T(8,128)(2,1)} %bitcast.12, bf16[128,1024]{1,0:T(8,128)(2,1)} %bitcast.13, bf16[6144,1024]{1,0:T(8,128)(2,1)} %w_hbm.1, ...), custom_call_target="tpu_custom_call" | custom-call | tf_op jit(solution)/shard_map/whole/pallas_call | solution.py:551
  98.5 1.6 %apart.1 = (f32[48,1024]{1,0:T(8,128)}, f32[8,1024]{1,0:T(8,128)}, f32[1,1024]{1,0:T(1,128)}, f32[1,8]{1,0:T(1,128)}) custom-call(f32[64,1024]{1,0:T(8,128)} %whole.1.out_ref), custom_call_target="tpu_custom_call" | custom-call | tf_op jit(solution)/shard_map/apart/pallas_call | solution.py:611

commit v8 on v7

--- a/solution.py
+++ b/solution.py
@@ -94,7 +94,7 @@
 
 
 def whole_body(dims, norm, per, tq, sub, order_ref, bias_ref, limit_ref, q_hbm, k_hbm, v_hbm, w_hbm, bin_ref, w2t_ref, out_ref,
-               feat, qa, ka, stage, wbuf, pre, pred_ref, slope_ref, act_ref, qs, ks, bufs, acc_ref, msort, mass_ref, f_ref,
+               feat, qa, ka, stage, wbuf, pre, pred_ref, slope_ref, act_ref, inv, qs, ks, bufs, acc_ref, msort, mass_ref, f_ref,
                mrecv, lab, dl, ft, part, pair, xrecv, sm, small, smr, zs, ys, xs,
                w_sem, in_sem, i_send, i_recv, d_send, d_recv, f_send, f_recv,
                m_send, m_recv, g_send, g_recv, p_send, p_recv, x_send, x_recv, s_send, s_recv):
@@ -170,7 +170,7 @@
     def across(i, to, frm):
         return remote(feat.at[:, parts(to)[i]], arrivals(frm)[i], i_send.at[i, to], i_recv.at[i, frm], (2 * to + core, b))
 
-    for some in ((1, 2), (0,)):
+    for some in ((1,), (2,), (0,)):
         for d in away:
             for i in some:
                 across(i, chip_at(d, 1), c).start()
@@ -181,6 +181,14 @@
 
     over(0, feat.at[:, other_q], c, core).start()
     over(1, feat.at[:, own_k], c, core).start()
+
+    def find(at, _):
+        stored = jnp.int32(0)
+        for k in range(1, n):
+            stored = stored + k * jnp.maximum(1 - jnp.abs(order_ref[k] - at), 0)
+        inv[at] = jnp.minimum(stored, n - 1)
+        return 0
+    lax.fori_loop(0, n, find, 0)
 
     def step(i, _):
         w_copy(i).wait()
@@ -232,11 +240,8 @@
         f_copy(chip_at(d, 1), c).start()
 
     def sort(at, _):
-        stored = jnp.int32(0)
-        for k in range(1, n):
-            stored = stored + k * jnp.maximum(1 - jnp.abs(order_ref[k] - at), 0)
         here = pl.ds(pl.multiple_of(at * rows, rows), rows)
-        stored = jnp.minimum(stored, n - 1)
+        stored = inv[at]
         qs[here, :] = qa[stored]
         ks[here, :] = ka[stored]
         return 0
@@ -563,6 +568,7 @@
             vm((heads, rows), f32),
             vm((rows, hidden), f32),
             vm((rows, hidden), bf16),
+            pltpu.SMEM((n,), jnp.int32),
             vm((n * rows, size), bf16),
             vm((n * rows, size), bf16),
             tuple(vm((n * rows, tq), f32) for _ in range(3)),

time: 100 us -> 99.6 us (level)
  no operation moved by 1% of the time
where the time goes in v8:
time: 99.6 us; the launch traced here: 99.4 us
  Pallas kernels  98.1 us (98%)
  between operations  1.29 us (1%)
    pallas_call x1, Pallas kernels, whole(): pl.pallas_call(functools.partial(whole_body, dims, norm, q.shape[1] // k....  96.4 us

profile of v8, /device:TPU:1, one launch (start us, length us, event | category | flops | bytes accessed | tf_op | source)
XLA Modules:
  0.0 99.4 jit_solution(2114116563822028061)
XLA Ops:
  1.3 96.4 %whole.1.out_ref = f32[64,1024]{1,0:T(8,128)} custom-call(s32[32]{0:T(128)} %bitcast.16, f32[8]{0:T(128)} %bias_ref.1, s32[1,1]{1,0:T(1,128)} %bitcast.10.limit_ref, bf16[128,4096]{1,0:T(8,128)(2,1)} %bitcast.11, bf16[128,1024]{1,0:T(8,128)(2,1)} %bitcast.12, bf16[128,1024]{1,0:T(8,128)(2,1)} %bitcast.13, bf16[6144,1024]{1,0:T(8,128)(2,1)} %w_hbm.1, ...), custom_call_target="tpu_custom_call" | custom-call | tf_op jit(solution)/shard_map/whole/pallas_call | solution.py:556
  97.7 1.6 %apart.1 = (f32[48,1024]{1,0:T(8,128)}, f32[8,1024]{1,0:T(8,128)}, f32[1,1024]{1,0:T(1,128)}, f32[1,8]{1,0:T(1,128)}) custom-call(f32[64,1024]{1,0:T(8,128)} %whole.1.out_ref), custom_call_target="tpu_custom_call" | custom-call | tf_op jit(solution)/shard_map/apart/pallas_call | solution.py:617

commit v9 on v8

--- a/solution.py
+++ b/solution.py
@@ -296,11 +296,12 @@
     live = jnp.where(position < limit_ref[...], 1.0, 0.0)
     resid_t = ((pred_ref[...] - lab[...]) * live * norm).astype(jnp.bfloat16)
     resid = resid_t.astype(jnp.float32).T.astype(jnp.bfloat16)
-    back = jnp.dot(resid, w2t_ref[...], preferred_element_type=jnp.float32)
-    delta = (back * slope_ref[...]).astype(jnp.bfloat16)
     here = pl.ds(pl.multiple_of(c * rows, rows), rows)
-    for j in range(chunks):
-        dl[j][here, :] = delta[:, begin[j]:begin[j + 1]]
+
+    def make(j):
+        cut = slice(begin[j], begin[j + 1])
+        back = jnp.dot(resid, w2t_ref[:, cut], preferred_element_type=jnp.float32)
+        dl[j][here, :] = (back * slope_ref[:, cut]).astype(jnp.bfloat16)
 
     wide = rows // 2
     slot = {}
@@ -438,7 +439,9 @@
     def small_start0():
         sw = sm.shape[2]
         out_term = jnp.dot(resid_t, act_ref[...], preferred_element_type=jnp.float32)
-        sums = jnp.sum(delta.astype(jnp.float32), axis=0, keepdims=True)
+        sums = jnp.concatenate(
+            [jnp.sum(d[here, :].astype(jnp.float32), axis=0, keepdims=True) for d in dl], axis=1
+        )
         bias = jnp.sum(resid.astype(jnp.float32), axis=0, keepdims=True)
         lanes = 128
         cols = [out_term[:, k * lanes:(k + 1) * lanes] for k in range(hidden // lanes)]
@@ -501,7 +504,9 @@
             out_ref[base:base + 1, k * lanes:(k + 1) * lanes] = small[1, k:k + 1, hidden - sw:hidden - sw + lanes]
         out_ref[base + 1:base + 2, :lanes] = small[1, 0:1, hidden - sw + lanes:hidden - sw + 2 * lanes]
 
+    make(0)
     stage0(0)
+    make(1)
     stage0(1)
     small_start0()
     stage1(0)

time: 99.6 us -> 99.6 us (level)
  no operation moved by 1% of the time
where the time goes in v9:
time: 99.6 us; the launch traced here: 99.3 us
  Pallas kernels  98 us (98%)
  between operations  1.29 us (1%)
    pallas_call x1, Pallas kernels, whole(): pl.pallas_call(functools.partial(whole_body, dims, norm, q.shape[1] // k....  96.4 us

profile of v9, /device:TPU:1, one launch (start us, length us, event | category | flops | bytes accessed | tf_op | source)
XLA Modules:
  0.0 99.3 jit_solution(9162965332903280334)
XLA Ops:
  1.3 96.4 %whole.1.out_ref = f32[64,1024]{1,0:T(8,128)} custom-call(s32[32]{0:T(128)} %bitcast.16, f32[8]{0:T(128)} %bias_ref.1, s32[1,1]{1,0:T(1,128)} %bitcast.10.limit_ref, bf16[128,4096]{1,0:T(8,128)(2,1)} %bitcast.11, bf16[128,1024]{1,0:T(8,128)(2,1)} %bitcast.12, bf16[128,1024]{1,0:T(8,128)(2,1)} %bitcast.13, bf16[6144,1024]{1,0:T(8,128)(2,1)} %w_hbm.1, ...), custom_call_target="tpu_custom_call" | custom-call | tf_op jit(solution)/shard_map/whole/pallas_call | solution.py:561
  97.7 1.6 %apart.1 = (f32[48,1024]{1,0:T(8,128)}, f32[8,1024]{1,0:T(8,128)}, f32[1,1024]{1,0:T(1,128)}, f32[1,8]{1,0:T(1,128)}) custom-call(f32[64,1024]{1,0:T(8,128)} %whole.1.out_ref), custom_call_target="tpu_custom_call" | custom-call | tf_op jit(solution)/shard_map/apart/pallas_call | solution.py:622
